TPU v7x, 32 devices: a whole 2x2x4 slice. The times are simulated.
32 devices in a mesh: gx: 4 (over y, x), gy: 8 (over z, core).
Axes of the slice: x: 2, y: 2, z: 4, core: 2. Of those that a mesh axis runs over, the one named last changes fastest.
Arguments:
- tile_flux: bfloat16 [4, 12, 8, 131072], P(None, None, None, ('gx', 'gy')), may hold values from -6 to 6
- tile_frac: float32 [8, 131072], P(None, ('gx', 'gy')), may hold values from 0.02 to 1
- weights: bfloat16 [32, 7, 16, 256, 128], P(('gx', 'gy')), may hold values from -0.049804688 to 0.14941406
- block_row: int32 [32, 7, 16], P(('gx', 'gy')), may hold values from 0 to 47
- block_col: int32 [32, 7, 16], P(('gx', 'gy')), may hold values from 0 to 31
- send_counts: int32 [32, 7], P(('gx', 'gy')), may hold values from 1 to 16, as said below
Outputs:
- atm_flux: float32 [4, 12, 393216], P(None, None, ('gx', 'gy'))
Inputs may be any that keep to these rules, and one draw needn't show every extreme that they name: `send_counts`: live slots of a device at an offset; some device has all 7 offsets at 16, and some device receives 16 live slots from every offset.
All inputs are finite; a program needn't handle non-finite values.
Results may differ from a plain program's by a relative error of at most 0.0029.
Values sent between devices are 32-bit elements; how exact they have to be, the bound alone decides.
No kernel may reach another device: no remote copies, remote signals or barrier semaphores. Data moves between devices by JAX's collectives and lax.ppermute only.
A program may use at most 128 MiB of HBM per device.

v0:
```python
import jax
import jax.numpy as jnp
from jax import lax
from jax.sharding import PartitionSpec as P

AB_DEV = 48


def shifted(value, axis, steps):
    count = lax.axis_size(axis)
    pairs = [(source, (source + steps) % count) for source in range(count)]
    return lax.ppermute(value, axis, pairs)


def settle(partial_value, targets, blocks_here):
    onehot = (targets[:, None] == jnp.arange(blocks_here, dtype=jnp.float32)[None, :]).astype(
        jnp.float32
    )
    return jnp.einsum("kj,kfr->jfr", onehot, partial_value, precision=lax.Precision.HIGHEST)


def on_device(tile_flux, tile_frac, weights, block_row, block_col, send_counts):
    num_steps = tile_flux.shape[0]
    num_kinds = tile_flux.shape[1]
    num_flux = num_steps * num_kinds
    num_off = weights.shape[1]
    slots = weights.shape[2]
    block_rows = weights.shape[3]
    block_cols = weights.shape[4]
    reach_side = num_off // 2
    frac_sum = jnp.sum(tile_frac, axis=0)
    merged = (
        jnp.sum(tile_flux.astype(jnp.float32) * tile_frac[None, None], axis=2) / frac_sum
    ).astype(jnp.bfloat16)
    land_blocks = merged.reshape(num_flux, -1, block_cols)
    picked = jnp.take(land_blocks, block_col[0].reshape(-1), axis=1)
    picked = picked.reshape(num_flux, num_off, slots, block_cols)
    partial_value = jnp.einsum(
        "okrc,fokc->okfr", weights[0], picked, preferred_element_type=jnp.float32
    )
    active = (jnp.arange(slots, dtype=jnp.int32)[None, :] < send_counts[0][:, None]).astype(
        jnp.float32
    )
    partial_value = partial_value * active[:, :, None, None]
    targets = block_row[0].astype(jnp.float32)
    totals = settle(partial_value[reach_side], targets[reach_side], AB_DEV)
    for offset in range(num_off):
        if offset != reach_side:
            arrived, arrived_rows = shifted(
                (partial_value[offset], targets[offset]), ("gx", "gy"), offset - reach_side
            )
            totals = totals + settle(arrived, arrived_rows, AB_DEV)
    return totals.transpose(1, 0, 2).reshape(num_steps, num_kinds, AB_DEV * block_rows)


def solution(mesh):
    return jax.shard_map(
        on_device,
        mesh=mesh,
        in_specs=(
            P(None, None, None, ("gx", "gy")),
            P(None, ("gx", "gy")),
            P(("gx", "gy"), None, None, None, None),
            P(("gx", "gy"), None, None),
            P(("gx", "gy"), None, None),
            P(("gx", "gy"), None),
        ),
        out_specs=P(None, None, ("gx", "gy")),
        check_vma=False,
    )
```

profile of v0, /device:TPU:0, one launch (start us, length us, event | category | flops | bytes accessed | tf_op | source)
XLA Modules:
  0.0 137.1 jit_solution(5694432180098506802)
XLA Ops:
  0.0 0.7 reduce
  0.7 0.1 reshape_squeeze.6
  0.8 0.8 fusion.45
  1.6 0.9 reduce_sum.22
  2.5 4.0 %multiply_reduce_fusion = f32[4,12,4096]{2,1,0:T(8,128)S(1)} fusion(bf16[4,12,8,4096]{3,2,1,0:T(8,128)(2,1)} %param.6, f32[8,4096]{1,0:T(8,128)} %param.7), kind=kLoop, calls=%fused_computation.3 | loop fusion | flops 4521984 | bytes 4063232 | tf_op jit(solution)/shard_map/reduce_sum | solution.py:33
  6.5 0.2 reduce_sum.21
  6.7 0.5 fusion.22
  7.2 0.8 gather_fusion
  8.0 5.8 %broadcast_multiply_fusion = f32[7,16,48,256]{3,2,1,0:T(8,128)S(1)} fusion(f32[7,16]{1,0:T(8,128)S(1)} %get-tuple-element.19, bf16[1,7,16,256,128]{4,3,2,1,0:T(8,128)(2,1)} %param.8, bf16[48,7,16,128]{3,0,2,1:T(8,128)(2,1)S(1)} %bitcast.67, pred[7,16]{1,0:T(8,128)(4,1)S(1)} %get-tuple-element.20), kind=kOutput, calls=%fused_computation.4 | convolution fusion | flops 354385920 | bytes 14221872 | tf_op jit(solution)/shard_map/okrc,fokc->okfr/dot_general | solution.py:38
  13.8 0.0 copy-start
  13.8 0.4 slice_bitcast_fusion
  14.2 5.4 %collective-permute-start.1 = (f32[16,48,256]{2,1,0:T(8,128)S(1)}, f32[16,48,256]{2,1,0:T(8,128)S(1)}, u32[]{:S(2)}, u32[]{:S(2)}) collective-permute-start(f32[16,48,256]{2,1,0:T(8,128)S(1)} %get-tuple-element.10), channel_id=1, source_target_pairs={{0,29},{1,30},{2,31},{3,0},{4,1},{5,2},{6,3},{7,4},{8,5},{9,6},{10... | collective-permute-start | bytes 2359304 | tf_op jit(solution)/shard_map/ppermute | solution.py:12
  19.7 1.6 %collective-permute-start.3 = (f32[16,48,256]{2,1,0:T(8,128)S(1)}, f32[16,48,256]{2,1,0:T(8,128)S(1)}, u32[]{:S(2)}, u32[]{:S(2)}) collective-permute-start(f32[16,48,256]{2,1,0:T(8,128)S(1)} %get-tuple-element.9), channel_id=1, source_target_pairs={{0,30},{1,31},{2,0},{3,1},{4,2},{5,3},{6,4},{7,5},{8,6},{9,7},{10,... | collective-permute-start | bytes 2359304 | tf_op jit(solution)/shard_map/ppermute | solution.py:12
  21.3 0.0 copy-done
  21.3 1.5 %collective-permute-start.10 = (f32[16]{0:T(128)S(1)}, f32[16]{0:T(128)S(1)}, u32[]{:S(2)}, u32[]{:S(2)}) collective-permute-start(f32[16]{0:T(128)S(1)} %get-tuple-element.12), channel_id=1, source_target_pairs={{0,3},{1,4},{2,5},{3,6},{4,7},{5,8},{6,9},{7,10},{8,11},{9,12},{10... | collective-permute-start | bytes 200 | tf_op jit(solution)/shard_map/ppermute | solution.py:12
  22.8 3.0 %collective-permute-start = (f32[16]{0:T(128)S(1)}, f32[16]{0:T(128)S(1)}, u32[]{:S(2)}, u32[]{:S(2)}) collective-permute-start(f32[16]{0:T(128)S(1)} %get-tuple-element.17), channel_id=1, source_target_pairs={{0,29},{1,30},{2,31},{3,0},{4,1},{5,2},{6,3},{7,4},{8,5},{9,6},{10... | collective-permute-start | bytes 200 | tf_op jit(solution)/shard_map/ppermute | solution.py:12
  25.8 0.0 collective-permute-start.5
  25.8 1.4 %fusion.20 = f32[48,48,256]{2,0,1:T(8,128)S(1)} fusion(f32[16,48,256]{2,1,0:T(8,128)S(1)} %get-tuple-element.11, f32[16]{0:T(128)S(1)} %get-tuple-element.18), kind=kOutput, calls=%fused_computation.27 | convolution fusion | flops 113246976 | bytes 3145792 | tf_op jit(solution)/shard_map/kj,kfr->jfr/dot_general | solution.py:19
  27.3 28.8 %collective-permute-done = f32[16]{0:T(128)S(1)} collective-permute-done((f32[16]{0:T(128)S(1)}, f32[16]{0:T(128)S(1)}, u32[]{:S(2)}, u32[]{:S(2)}) %collective-permute-start) | collective-permute-done | bytes 96 | tf_op jit(solution)/shard_map/ppermute | solution.py:12
  56.1 5.6 %collective-permute-start.2 = (f32[16]{0:T(128)S(1)}, f32[16]{0:T(128)S(1)}, u32[]{:S(2)}, u32[]{:S(2)}) collective-permute-start(f32[16]{0:T(128)S(1)} %get-tuple-element.16), channel_id=1, source_target_pairs={{0,30},{1,31},{2,0},{3,1},{4,2},{5,3},{6,4},{7,5},{8,6},{9,7},{10,... | collective-permute-start | bytes 200 | tf_op jit(solution)/shard_map/ppermute | solution.py:12
  61.6 0.0 collective-permute-done.1
  61.6 15.5 %collective-permute-start.7 = (f32[16,48,256]{2,1,0:T(8,128)S(1)}, f32[16,48,256]{2,1,0:T(8,128)S(1)}, u32[]{:S(2)}, u32[]{:S(2)}) collective-permute-start(f32[16,48,256]{2,1,0:T(8,128)S(1)} %get-tuple-element.7), channel_id=1, source_target_pairs={{0,1},{1,2},{2,3},{3,4},{4,5},{5,6},{6,7},{7,8},{8,9},{9,10},{10,1... | collective-permute-start | bytes 2359304 | tf_op jit(solution)/shard_map/ppermute | solution.py:12
  77.1 1.4 %fusion.18 = f32[48,48,256]{2,0,1:T(8,128)S(1)} fusion(f32[16,48,256]{2,1,0:T(8,128)S(1)} %collective-permute-done.1, f32[16]{0:T(128)S(1)} %collective-permute-done), kind=kOutput, calls=%fused_computation.25 | convolution fusion | flops 113246976 | bytes 3145792 | tf_op jit(solution)/shard_map/kj,kfr->jfr/dot_general | solution.py:19
  78.6 0.0 collective-permute-done.2
  78.6 4.5 %collective-permute-start.4 = (f32[16]{0:T(128)S(1)}, f32[16]{0:T(128)S(1)}, u32[]{:S(2)}, u32[]{:S(2)}) collective-permute-start(f32[16]{0:T(128)S(1)} %get-tuple-element.15), channel_id=1, source_target_pairs={{0,31},{1,0},{2,1},{3,2},{4,3},{5,4},{6,5},{7,6},{8,7},{9,8},{10,9... | collective-permute-start | bytes 200 | tf_op jit(solution)/shard_map/ppermute | solution.py:12
  83.0 0.0 collective-permute-done.3
  83.1 0.0 collective-permute-start.9
  83.1 1.4 %fusion.16 = f32[48,48,256]{2,0,1:T(8,128)S(1)} fusion(f32[16,48,256]{2,1,0:T(8,128)S(1)} %collective-permute-done.3, f32[16]{0:T(128)S(1)} %collective-permute-done.2), kind=kOutput, calls=%fused_computation.23 | convolution fusion | flops 113246976 | bytes 3145792 | tf_op jit(solution)/shard_map/kj,kfr->jfr/dot_general | solution.py:19
  84.5 0.0 collective-permute-done.4
  84.5 0.1 collective-permute-start.6
  84.6 0.0 collective-permute-done.5
  84.6 0.2 collective-permute-start.11
  84.8 1.4 %fusion.14 = f32[48,48,256]{2,0,1:T(8,128)S(1)} fusion(f32[16,48,256]{2,1,0:T(8,128)S(1)} %collective-permute-done.5, f32[16]{0:T(128)S(1)} %collective-permute-done.4), kind=kOutput, calls=%fused_computation.21 | convolution fusion | flops 113246976 | bytes 3145792 | tf_op jit(solution)/shard_map/kj,kfr->jfr/dot_general | solution.py:19
  86.3 13.9 %collective-permute-done.6 = f32[16]{0:T(128)S(1)} collective-permute-done((f32[16]{0:T(128)S(1)}, f32[16]{0:T(128)S(1)}, u32[]{:S(2)}, u32[]{:S(2)}) %collective-permute-start.6) | collective-permute-done | bytes 96 | tf_op jit(solution)/shard_map/ppermute | solution.py:12
  100.2 7.0 %collective-permute-start.8 = (f32[16]{0:T(128)S(1)}, f32[16]{0:T(128)S(1)}, u32[]{:S(2)}, u32[]{:S(2)}) collective-permute-start(f32[16]{0:T(128)S(1)} %get-tuple-element.13), channel_id=1, source_target_pairs={{0,2},{1,3},{2,4},{3,5},{4,6},{5,7},{6,8},{7,9},{8,10},{9,11},{10,... | collective-permute-start | bytes 200 | tf_op jit(solution)/shard_map/ppermute | solution.py:12
  107.1 0.0 collective-permute-done.7
  107.2 1.4 %fusion.12 = f32[48,48,256]{2,0,1:T(8,128)S(1)} fusion(f32[16,48,256]{2,1,0:T(8,128)S(1)} %collective-permute-done.7, f32[16]{0:T(128)S(1)} %collective-permute-done.6), kind=kOutput, calls=%fused_computation.19 | convolution fusion | flops 113246976 | bytes 3145792 | tf_op jit(solution)/shard_map/kj,kfr->jfr/dot_general | solution.py:19
  108.6 11.9 %collective-permute-done.8 = f32[16]{0:T(128)S(1)} collective-permute-done((f32[16]{0:T(128)S(1)}, f32[16]{0:T(128)S(1)}, u32[]{:S(2)}, u32[]{:S(2)}) %collective-permute-start.8) | collective-permute-done | bytes 96 | tf_op jit(solution)/shard_map/ppermute | solution.py:12
  120.5 0.0 collective-permute-done.9
  120.5 1.4 %fusion.10 = f32[48,48,256]{2,0,1:T(8,128)S(1)} fusion(f32[16,48,256]{2,1,0:T(8,128)S(1)} %collective-permute-done.9, f32[16]{0:T(128)S(1)} %collective-permute-done.8), kind=kOutput, calls=%fused_computation.17 | convolution fusion | flops 113246976 | bytes 3145792 | tf_op jit(solution)/shard_map/kj,kfr->jfr/dot_general | solution.py:19
  122.0 0.0 collective-permute-done.10
  122.0 6.9 %collective-permute-done.11 = f32[16,48,256]{2,1,0:T(8,128)S(1)} collective-permute-done((f32[16,48,256]{2,1,0:T(8,128)S(1)}, f32[16,48,256]{2,1,0:T(8,128)S(1)}, u32[]{:S(2)}, u32[]{:S(2)}) %collective-permute-start.11) | collective-permute-done | bytes 786464 | tf_op jit(solution)/shard_map/ppermute | solution.py:12
  128.9 3.4 %add_bitcast_fusion = f32[48,48,256]{2,1,0:T(8,128)} fusion(f32[48,48,256]{2,0,1:T(8,128)S(1)} %fusion.10, f32[48,48,256]{2,0,1:T(8,128)S(1)} %fusion.12, f32[48,48,256]{2,0,1:T(8,128)S(1)} %fusion.14, f32[48,48,256]{2,0,1:T(8,128)S(1)} %fusion.16, f32[48,48,256]{2,0,1:T(8,128)S(1)} %fusion.20, f32[48,48,256]{2,0,1:T(8,128)S(1)} %fusion.18, ...), kind=kOutput, calls=%fused_computation.5 | convolution fusion | flops 116785920 | bytes 17301568 | tf_op jit(solution)/shard_map/kj,kfr->jfr/dot_general | solution.py:19
  132.3 1.9 %reshape.94 = f32[4,12,12288]{2,1,0:T(8,128)S(1)} reshape(f32[48,48,256]{2,1,0:T(8,128)} %add_bitcast_fusion) | data formatting | bytes 4718592 | tf_op jit(solution)/shard_map/reshape | solution.py:53
  134.2 2.9 %copy.23 = f32[4,12,12288]{2,0,1:T(4,128)} copy(f32[4,12,12288]{2,1,0:T(8,128)S(1)} %reshape.94) | data formatting | bytes 4718592 | tf_op jit(solution)/shard_map/reshape | solution.py:53
  (4 shorter events, 0.0 us)
Async XLA Ops:
  13.8 7.5 %copy-start = (s32[1,7,16]{2,0,1:T(1,128)S(1)}, s32[1,7,16]{2,0,1:T(1,128)}, u32[]{:S(2)}) copy-start(s32[1,7,16]{2,0,1:T(1,128)} %param.9) | copy-start | bytes 1348
  14.2 47.4 %collective-permute-start.1 = (f32[16,48,256]{2,1,0:T(8,128)S(1)}, f32[16,48,256]{2,1,0:T(8,128)S(1)}, u32[]{:S(2)}, u32[]{:S(2)}) collective-permute-start(f32[16,48,256]{2,1,0:T(8,128)S(1)} %get-tuple-element.10), channel_id=1, source_target_pairs={{0,29},{1,30},{2,31},{3,0},{4,1},{5,2},{6,3},{7,4},{8,5},{9,6},{10... | collective-permute-start | bytes 2359304 | tf_op jit(solution)/shard_map/ppermute | solution.py:12
  19.7 63.4 %collective-permute-start.3 = (f32[16,48,256]{2,1,0:T(8,128)S(1)}, f32[16,48,256]{2,1,0:T(8,128)S(1)}, u32[]{:S(2)}, u32[]{:S(2)}) collective-permute-start(f32[16,48,256]{2,1,0:T(8,128)S(1)} %get-tuple-element.9), channel_id=1, source_target_pairs={{0,30},{1,31},{2,0},{3,1},{4,2},{5,3},{6,4},{7,5},{8,6},{9,7},{10,... | collective-permute-start | bytes 2359304 | tf_op jit(solution)/shard_map/ppermute | solution.py:12
  21.3 100.6 %collective-permute-start.10 = (f32[16]{0:T(128)S(1)}, f32[16]{0:T(128)S(1)}, u32[]{:S(2)}, u32[]{:S(2)}) collective-permute-start(f32[16]{0:T(128)S(1)} %get-tuple-element.12), channel_id=1, source_target_pairs={{0,3},{1,4},{2,5},{3,6},{4,7},{5,8},{6,9},{7,10},{8,11},{9,12},{10... | collective-permute-start | bytes 200 | tf_op jit(solution)/shard_map/ppermute | solution.py:12
  22.8 33.3 %collective-permute-start = (f32[16]{0:T(128)S(1)}, f32[16]{0:T(128)S(1)}, u32[]{:S(2)}, u32[]{:S(2)}) collective-permute-start(f32[16]{0:T(128)S(1)} %get-tuple-element.17), channel_id=1, source_target_pairs={{0,29},{1,30},{2,31},{3,0},{4,1},{5,2},{6,3},{7,4},{8,5},{9,6},{10... | collective-permute-start | bytes 200 | tf_op jit(solution)/shard_map/ppermute | solution.py:12
  25.8 58.7 %collective-permute-start.5 = (f32[16,48,256]{2,1,0:T(8,128)S(1)}, f32[16,48,256]{2,1,0:T(8,128)S(1)}, u32[]{:S(2)}, u32[]{:S(2)}) collective-permute-start(f32[16,48,256]{2,1,0:T(8,128)S(1)} %get-tuple-element.8), channel_id=1, source_target_pairs={{0,31},{1,0},{2,1},{3,2},{4,3},{5,4},{6,5},{7,6},{8,7},{9,8},{10,9... | collective-permute-start | bytes 2359304 | tf_op jit(solution)/shard_map/ppermute | solution.py:12
  56.1 22.5 %collective-permute-start.2 = (f32[16]{0:T(128)S(1)}, f32[16]{0:T(128)S(1)}, u32[]{:S(2)}, u32[]{:S(2)}) collective-permute-start(f32[16]{0:T(128)S(1)} %get-tuple-element.16), channel_id=1, source_target_pairs={{0,30},{1,31},{2,0},{3,1},{4,2},{5,3},{6,4},{7,5},{8,6},{9,7},{10,... | collective-permute-start | bytes 200 | tf_op jit(solution)/shard_map/ppermute | solution.py:12
  61.6 45.5 %collective-permute-start.7 = (f32[16,48,256]{2,1,0:T(8,128)S(1)}, f32[16,48,256]{2,1,0:T(8,128)S(1)}, u32[]{:S(2)}, u32[]{:S(2)}) collective-permute-start(f32[16,48,256]{2,1,0:T(8,128)S(1)} %get-tuple-element.7), channel_id=1, source_target_pairs={{0,1},{1,2},{2,3},{3,4},{4,5},{5,6},{6,7},{7,8},{8,9},{9,10},{10,1... | collective-permute-start | bytes 2359304 | tf_op jit(solution)/shard_map/ppermute | solution.py:12
  78.6 5.9 %collective-permute-start.4 = (f32[16]{0:T(128)S(1)}, f32[16]{0:T(128)S(1)}, u32[]{:S(2)}, u32[]{:S(2)}) collective-permute-start(f32[16]{0:T(128)S(1)} %get-tuple-element.15), channel_id=1, source_target_pairs={{0,31},{1,0},{2,1},{3,2},{4,3},{5,4},{6,5},{7,6},{8,7},{9,8},{10,9... | collective-permute-start | bytes 200 | tf_op jit(solution)/shard_map/ppermute | solution.py:12
  83.1 37.5 %collective-permute-start.9 = (f32[16,48,256]{2,1,0:T(8,128)S(1)}, f32[16,48,256]{2,1,0:T(8,128)S(1)}, u32[]{:S(2)}, u32[]{:S(2)}) collective-permute-start(f32[16,48,256]{2,1,0:T(8,128)S(1)} %get-tuple-element.6), channel_id=1, source_target_pairs={{0,2},{1,3},{2,4},{3,5},{4,6},{5,7},{6,8},{7,9},{8,10},{9,11},{10,... | collective-permute-start | bytes 2359304 | tf_op jit(solution)/shard_map/ppermute | solution.py:12
  84.5 15.7 %collective-permute-start.6 = (f32[16]{0:T(128)S(1)}, f32[16]{0:T(128)S(1)}, u32[]{:S(2)}, u32[]{:S(2)}) collective-permute-start(f32[16]{0:T(128)S(1)} %get-tuple-element.14), channel_id=1, source_target_pairs={{0,1},{1,2},{2,3},{3,4},{4,5},{5,6},{6,7},{7,8},{8,9},{9,10},{10,1... | collective-permute-start | bytes 200 | tf_op jit(solution)/shard_map/ppermute | solution.py:12
  84.6 44.3 %collective-permute-start.11 = (f32[16,48,256]{2,1,0:T(8,128)S(1)}, f32[16,48,256]{2,1,0:T(8,128)S(1)}, u32[]{:S(2)}, u32[]{:S(2)}) collective-permute-start(f32[16,48,256]{2,1,0:T(8,128)S(1)} %get-tuple-element.5), channel_id=1, source_target_pairs={{0,3},{1,4},{2,5},{3,6},{4,7},{5,8},{6,9},{7,10},{8,11},{9,12},{10... | collective-permute-start | bytes 2359304 | tf_op jit(solution)/shard_map/ppermute | solution.py:12
  100.2 20.4 %collective-permute-start.8 = (f32[16]{0:T(128)S(1)}, f32[16]{0:T(128)S(1)}, u32[]{:S(2)}, u32[]{:S(2)}) collective-permute-start(f32[16]{0:T(128)S(1)} %get-tuple-element.13), channel_id=1, source_target_pairs={{0,2},{1,3},{2,4},{3,5},{4,6},{5,7},{6,8},{7,9},{8,10},{9,11},{10,... | collective-permute-start | bytes 200 | tf_op jit(solution)/shard_map/ppermute | solution.py:12
where the time goes:
time: 137 us
  waiting for transfers between devices  61.6 us (45%)
  starting transfers between devices  44.4 us (32%)
  matrix products  17.8 us (13%)
  other arithmetic  6.87 us (5%)
  local copies, waits for them, and re-layouts  6.33 us (5%)
    ppermute x12, waiting for transfers between devices, shifted(): return lax.ppermute(value, axis, pairs)  61.6 us
    ppermute x12, starting transfers between devices, shifted(): return lax.ppermute(value, axis, pairs)  44.4 us
    dot_general x7, matrix products, settle(): jnp.einsum('kj,kfr->jfr', onehot, partial_value, precision=lax.Precision....  12 us
    dot_general x1, matrix products, on_device(): jnp.einsum('okrc,fokc->okfr', weights[0], picked, preferred_element_type=...  5.81 us
    reshape x2, local copies, waits for them, and re-layouts, on_device(): totals.transpose(1, 0, 2).reshape(num_steps, num_kinds, AB_DEV * block_rows)  4.82 us
    reduce_sum x1, other arithmetic, on_device(): jnp.sum(tile_flux.astype(jnp.float32) * tile_frac[None, None], axis=2)  3.97 us
  transfers between devices with their start and end apart: 12, of which 4 were waited for; matrix products, arithmetic and copies ran while one was open for 6% of the time, Pallas kernels for 0%

commit v1 on v0

v1 whole, which is shorter than its diff:
```python
import functools
import itertools

import jax
import jax.numpy as jnp
from jax import lax
from jax.experimental import pallas as pl
from jax.experimental.pallas import tpu as pltpu
from jax.sharding import PartitionSpec as P


AXES = ("gx", "gy")
AB_DEV = 48
LANES = 128
SUBLANES = 8


def fold_rows(parts):
    row = lax.broadcasted_iota(jnp.int32, parts[0].shape, 0)
    step = SUBLANES // 2
    while step >= 1:
        low = (row // step) % 2 == 0
        half = len(parts) // 2
        merged = []
        for index in range(half):
            first, second = parts[index], parts[index + half]
            keep = jnp.where(low, first, second)
            swap = jnp.where(low, second, first)
            merged.append(keep + jnp.where(low, pltpu.roll(first, SUBLANES - step, 0), pltpu.roll(second, step, 0)))
            del swap
        parts = merged
        step //= 2
    return parts[0]


def merge_blocks(flux_ref, frac_ref, land_ref, first, count):
    steps, kinds = flux_ref.shape[0], flux_ref.shape[1]
    rows = steps * kinds

    @pl.loop(0, count, unroll=2)
    def _(index):
        lanes = pl.ds(pl.multiple_of(index * LANES, LANES), LANES)
        frac = frac_ref[:, pl.ds(pl.multiple_of((first + index) * LANES, LANES), LANES)]
        total = jnp.sum(frac, axis=0, keepdims=True)
        for pair in range(rows // (2 * SUBLANES)):
            pieces = []
            for half in range(2):
                parts = []
                for r in range(SUBLANES):
                    line = (2 * pair + half) * SUBLANES + r
                    parts.append(flux_ref[line % steps, line // steps, :, lanes].astype(jnp.float32) * frac)
                pieces.append(fold_rows(parts) / total)
            value = jnp.concatenate(pieces, axis=0).astype(jnp.bfloat16)
            land_ref[first + index, pl.ds(pair * 2 * SUBLANES, 2 * SUBLANES), :] = value


def block_product(land_ref, col, w_ref, local):
    return lax.dot_general(
        land_ref[col], w_ref[0, 0, local], (((1,), (1,)), ((), ())), preferred_element_type=jnp.float32
    )


def first_kernel(offs_ref, cols_ref, counts_ref, flux, frac, weights, land_out, *refs, entries, ranks):
    far = len(entries)
    outs, refs = refs[: far + ranks], refs[far + ranks :]
    flux_v, frac_v, w_v, land_v, near_v, piece_v, in_sems, w_sems, out_sems = refs
    groups, half = flux_v.shape[0], w_v.shape[1]
    wide = flux_v.shape[-1]
    piece = piece_v.shape[2]
    blocks = land_v.shape[0] // groups

    def load_flux(i):
        return pltpu.make_async_copy(flux.at[:, :, :, pl.ds(i * wide, wide)], flux_v.at[i], in_sems.at[1 + i])

    def load_weights(index, part):
        source = weights.at[0, offs_ref[entries[index]], pl.ds(part * half, half)]
        return pltpu.make_async_copy(source, w_v.at[part * far + index], w_sems.at[part * far + index])

    def crowded(index):
        return counts_ref[0, offs_ref[entries[index]]] > half

    load_frac = pltpu.make_async_copy(frac, frac_v, in_sems.at[0])
    load_frac.start()
    for i in range(groups):
        load_flux(i).start()
    for index in range(far):
        load_weights(index, 0).start()
    for index in range(far):

        @pl.when(crowded(index))
        def _():
            load_weights(index, 1).start()

    load_frac.wait()
    for i in range(groups):
        load_flux(i).wait()
        merge_blocks(flux_v.at[i], frac_v, land_v, i * blocks, blocks)
    stores = [pltpu.make_async_copy(land_v, land_out, out_sems.at[far + ranks])]
    stores[0].start()
    for index, entry in enumerate(entries):
        load_weights(index, 0).wait()
        for local in range(half):
            near_v[index, local] = lax.dot_general(
                land_v[cols_ref[offs_ref[entry], 0, local]],
                w_v[index, local],
                (((1,), (1,)), ((), ())),
                preferred_element_type=jnp.float32,
            )
        stores.append(pltpu.make_async_copy(near_v.at[index], outs[index], out_sems.at[index]))
        stores[-1].start()
    for index, entry in enumerate(entries):

        @pl.when(crowded(index))
        def _():
            load_weights(index, 1).wait()
            for local in range(half):
                piece_v[local // piece, index, local % piece] = lax.dot_general(
                    land_v[cols_ref[offs_ref[entry], 0, half + local]],
                    w_v[far + index, local],
                    (((1,), (1,)), ((), ())),
                    preferred_element_type=jnp.float32,
                )

    for k in range(ranks):
        stores.append(pltpu.make_async_copy(piece_v.at[k], outs[far + k], out_sems.at[far + k]))
        stores[-1].start()
    for store in stores:
        store.wait()


def first_products(tables, tile_flux, tile_frac, weights, entries, ranks, piece):
    steps, kinds, tiles, cells = tile_flux.shape
    _, _, slots, rows, cols = weights.shape
    nf, blocks, half, far = steps * kinds, cells // cols, slots // 2, len(entries)
    groups = min(g for g in range(1, blocks + 1) if blocks % g == 0 and blocks // g <= 4)
    anywhere = pl.BlockSpec(memory_space=pl.ANY)
    return pl.pallas_call(
        functools.partial(first_kernel, entries=entries, ranks=ranks),
        in_specs=[pl.BlockSpec(memory_space=pltpu.SMEM)] * 3 + [anywhere] * 3,
        out_specs=[anywhere] * (1 + far + ranks),
        out_shape=[jax.ShapeDtypeStruct((blocks, nf, cols), jnp.bfloat16)]
        + [jax.ShapeDtypeStruct((half, nf, rows), jnp.float32) for _ in entries]
        + [jax.ShapeDtypeStruct((far, piece, nf, rows), jnp.float32) for _ in range(ranks)],
        scratch_shapes=[
            pltpu.VMEM((groups, steps, kinds, tiles, cells // groups), tile_flux.dtype),
            pltpu.VMEM(tile_frac.shape, tile_frac.dtype),
            pltpu.VMEM((2 * far, half, rows, cols), weights.dtype),
            pltpu.VMEM((blocks, nf, cols), jnp.bfloat16),
            pltpu.VMEM((far, half, nf, rows), jnp.float32),
            pltpu.VMEM((ranks, far, piece, nf, rows), jnp.float32),
            pltpu.SemaphoreType.DMA((1 + groups,)),
            pltpu.SemaphoreType.DMA((2 * far,)),
            pltpu.SemaphoreType.DMA((far + ranks + 1,)),
        ],
        name="first",
    )(*tables, tile_flux, tile_frac, weights)


def product_kernel(offs_ref, cols_ref, counts_ref, land_ref, *refs, chunks):
    for index, (entry, first) in enumerate(chunks):
        w_ref = refs[index]
        out_ref = refs[len(chunks) + index]
        offset = offs_ref[entry]
        for start in range(0, out_ref.shape[0], SUBLANES):

            @pl.when(first + start < counts_ref[0, offset])
            def _():
                for local in range(start, min(start + SUBLANES, out_ref.shape[0])):
                    out_ref[local] = block_product(land_ref, cols_ref[offset, 0, first + local], w_ref, local)


def products(tables, land, weights, chunks, width):
    _, _, _, rows, cols = weights.shape
    blocks, nf, _ = land.shape
    return pl.pallas_call(
        functools.partial(product_kernel, chunks=chunks),
        grid_spec=pltpu.PrefetchScalarGridSpec(
            num_scalar_prefetch=3,
            grid=(1,),
            in_specs=[pl.BlockSpec((blocks, nf, cols), lambda i, *_: (0, 0, 0))]
            + [
                pl.BlockSpec((1, 1, width, rows, cols), lambda i, offs, *_, e=e, f=f: (0, offs[e], f // width, 0, 0))
                for e, f in chunks
            ],
            out_specs=[pl.BlockSpec((width, nf, rows), lambda i, *_: (0, 0, 0)) for _ in chunks],
        ),
        out_shape=[jax.ShapeDtypeStruct((width, nf, rows), jnp.float32) for _ in chunks],
        name="products",
    )(*tables, land, *([weights] * len(chunks)))


def choose_kernel(offs_ref, counts_ref, *refs, entries, half):
    ranks = len(refs) - 1 - len(entries)
    outs, sems = refs[ranks:-1], refs[-1]
    for go in (True, False):
        for index, entry in enumerate(entries):
            pick = jnp.int32(0)
            for rank in reversed(range(ranks)):
                pick = jnp.where(counts_ref[rank, offs_ref[entry]] > half, rank, pick)
            for rank in range(ranks):

                @pl.when(pick == rank)
                def _():
                    copy = pltpu.make_async_copy(refs[rank].at[index], outs[index], sems.at[index])
                    copy.start() if go else copy.wait()


def choose(offs, counts, givens, entries, half):
    return pl.pallas_call(
        functools.partial(choose_kernel, entries=entries, half=half),
        in_specs=[pl.BlockSpec(memory_space=pltpu.SMEM)] * 2 + [pl.BlockSpec(memory_space=pl.ANY)] * len(givens),
        out_specs=[pl.BlockSpec(memory_space=pltpu.VMEM)] * len(entries),
        out_shape=[jax.ShapeDtypeStruct(givens[0].shape[1:], jnp.float32)] * len(entries),
        scratch_shapes=[pltpu.SemaphoreType.DMA((len(entries),))],
        name="choose",
    )(offs, counts, *givens)


def pack_kernel(*refs):
    givens, out, sems = refs[:-2], refs[-2], refs[-1]
    copies = [pltpu.make_async_copy(g, out.at[i], sems.at[i]) for i, g in enumerate(givens)]
    for copy in copies:
        copy.start()
    for copy in copies:
        copy.wait()


def pack(givens):
    return pl.pallas_call(
        pack_kernel,
        in_specs=[pl.BlockSpec(memory_space=pl.ANY)] * len(givens),
        out_specs=pl.BlockSpec(memory_space=pltpu.VMEM),
        out_shape=jax.ShapeDtypeStruct((len(givens), *givens[0].shape), jnp.float32),
        scratch_shapes=[pltpu.SemaphoreType.DMA((len(givens),))],
        name="pack",
    )(*givens)


def settle_kernel(rows_ref, *refs, entries, count, fresh):
    rest = refs[count:]
    given = None if fresh else rest[0]
    out, totals, held, sems, moves = rest[-5:]
    last = rows_ref.shape[0] - 1

    def live(entry):
        _, _, row, first, limit, _, fast = entries[entry]
        number = jnp.clip(rows_ref[row, 0] - first, 0, limit)
        return jnp.where(rows_ref[last, 0] > 0, 0, number) if fast else number

    def copy(entry, slot):
        index, sub, place = entries[entry][0], entries[entry][1], entries[entry][5]
        source = refs[index].at[slot] if sub is None else refs[index].at[sub, slot]
        return pltpu.make_async_copy(source, held.at[place + slot], sems.at[place + slot])

    for entry in range(len(entries)):

        @pl.loop(0, live(entry))
        def _(slot, entry=entry):
            copy(entry, slot).start()

    if fresh:
        totals[...] = jnp.zeros(totals.shape, totals.dtype)
    else:
        load = pltpu.make_async_copy(given, totals, moves.at[0])
        load.start()
        load.wait()
    kinds = totals.shape[0]
    steps = totals.shape[2] // 2
    low = lax.broadcasted_iota(jnp.int32, (2 * steps, LANES), 0) < steps
    for entry in range(len(entries)):

        @pl.loop(0, live(entry))
        def _(slot, entry=entry):
            copy(entry, slot).wait()
            _, _, row, first, _, start, _ = entries[entry]
            block = rows_ref[row, 1 + first + slot]
            for pair in range(kinds // 2):
                lines = pl.ds(pair * 2 * steps, 2 * steps)
                left = held[start + slot, lines, pl.ds(0, LANES)]
                right = held[start + slot, lines, pl.ds(LANES, LANES)]
                totals[2 * pair, block] += jnp.where(low, left, pltpu.roll(right, steps, 0))
                totals[2 * pair + 1, block] += jnp.where(low, pltpu.roll(left, steps, 0), right)

    store = pltpu.make_async_copy(totals, out, moves.at[1])
    store.start()
    store.wait()


def settle(rows, parts, shape, totals=None):
    fresh = totals is None
    arrays = [array for array, _ in parts]
    entries, place = [], 0
    for index, (array, given) in enumerate(parts):
        for sub, (row, first, fast) in enumerate(given):
            width = array.shape[-3]
            entries.append((index, sub if array.ndim == 4 else None, row, first, width, place, fast))
            place += width
    count = len(arrays)
    given = [] if fresh else [totals]
    return pl.pallas_call(
        functools.partial(settle_kernel, entries=tuple(entries), count=count, fresh=fresh),
        in_specs=[pl.BlockSpec(memory_space=pltpu.SMEM)]
        + [pl.BlockSpec(memory_space=pl.ANY) for _ in arrays]
        + [pl.BlockSpec(memory_space=pl.ANY) for _ in given],
        out_specs=pl.BlockSpec(memory_space=pl.ANY),
        out_shape=jax.ShapeDtypeStruct(shape, jnp.float32),
        scratch_shapes=[
            pltpu.VMEM(shape, jnp.float32),
            pltpu.VMEM((place, *arrays[0].shape[-2:]), jnp.float32),
            pltpu.SemaphoreType.DMA((place,)),
            pltpu.SemaphoreType.DMA((2,)),
        ],
        input_output_aliases={} if fresh else {1 + count: 0},
        name="settle",
    )(rows, *arrays, *given)


def spread(held, axis, paired=False):
    size = lax.axis_size(axis)
    held = held[None]
    span = 1
    while span < size:
        pairs = [(d, d ^ span if paired else (d + span) % size) for d in range(size)]
        got = lax.ppermute(held, axis, pairs)
        held = jnp.concatenate([held, got], axis=0)
        span *= 2
    return held


def place_of(axis, other, paired=False):
    own = lax.axis_index(axis)
    return own ^ other if paired else (own - other) % lax.axis_size(axis)


def partners(reach):
    group = reach + 1
    period = 2 * group
    inner = [[(p ^ x) - p for x in range(1, group)] for p in range(period)]
    options = []
    for picked in itertools.permutations(range(group, period)):
        shifts = [next((v for v in (b - a, b - a - period) if abs(v) <= reach), None) for a, b in enumerate(picked)]
        if None not in shifts:
            options.append((abs(sum(1 if v > 0 else -1 for v in shifts)), shifts))
    options.sort(key=lambda option: option[0])
    for found in itertools.combinations([shifts for _, shifts in options], reach):
        if all(len({shifts[a] for shifts in found}) == reach for a in range(group)):
            break
    outer = [[0] * reach for _ in range(period)]
    for index, shifts in enumerate(found):
        for a, v in enumerate(shifts):
            outer[a][index] = v
            outer[(a + v) % period][index] = -v
    return [a + b for a, b in zip(inner, outer)]


def on_device(tile_flux, tile_frac, weights, block_row, block_col, send_counts):
    steps, kinds = tile_flux.shape[0], tile_flux.shape[1]
    _, num_off, slots, block_rows, _ = weights.shape
    ranks, line = lax.axis_size("gx"), lax.axis_size("gy")
    rank, here = lax.axis_index("gx"), lax.axis_index("gy")
    count = ranks * line
    half = slots // 2
    piece = -(-half // ranks)
    reach = num_off // 2
    shape = (kinds, AB_DEV, 2 * steps, block_rows // 2)
    shifts = partners(reach)
    period = len(shifts)
    near = tuple(range(reach))
    far = tuple(range(reach, 2 * reach))
    shift_here = jnp.array([row + [0] for row in shifts], jnp.int32)[here % period]
    offs = shift_here + reach
    tables = (offs, block_col.transpose(1, 0, 2), send_counts)

    def exchange(value, entry):
        return lax.ppermute(value, AXES, [(d, (d + shifts[d % period][entry]) % count) for d in range(count)])

    def across(value, step, back=False):
        pairs = [(r, (r + step) % ranks) for r in range(ranks)]
        return lax.ppermute(value, "gx", [(b, a) for a, b in pairs] if back else pairs)

    codes = jnp.where(jnp.arange(slots)[None, :] < send_counts[0][:, None], block_row[0], -1)
    family = spread(codes, "gx")
    numbers = jnp.sum(family[:ranks] >= 0, axis=2, dtype=jnp.int32)
    outside = jnp.any(jnp.arange(num_off)[:, None] == offs[None, reach : 2 * reach], axis=1)
    crowded = jnp.any((jnp.sum(numbers > half, axis=0) > 1) & outside)
    family = jnp.where(crowded & (family >= 0), family + AB_DEV, family)

    land, *given = first_products(tables, tile_flux, tile_frac, weights, far, ranks, piece)
    outer, parts = given[: len(far)], given[len(far) :]
    middle = near[1:2]
    inner = {}
    for those in (middle, tuple(e for e in near if e not in middle)):
        inner.update(zip(those, products(tables, land, weights, tuple((e, 0) for e in those), slots)))

    got = {e: exchange(outer[e - reach], e) for e in far}
    lent = [parts[0]] + [across(parts[k], k) for k in range(1, ranks)]
    got.update({e: exchange(inner[e], e) for e in near})
    relay = choose(offs, numbers, lent, far, half)
    passed = [exchange(r, e) for r, e in zip(relay, far)]
    paired = line & (line - 1) == 0
    held = spread(family, "gy", paired)

    sender = (rank * line + here + shift_here) % count
    back_offs = num_off - 1 - offs
    rows = held[place_of("gy", sender % line, paired), place_of("gx", sender // line), back_offs]
    flag = jnp.any(held >= AB_DEV).astype(jnp.int32)
    lives = jnp.sum(rows >= 0, axis=1, keepdims=True, dtype=jnp.int32)
    rows = jnp.concatenate([lives, rows % AB_DEV], axis=1)
    rows = jnp.concatenate([rows, jnp.broadcast_to(flag, (1, rows.shape[1]))], axis=0)

    (mine,) = products(tables, land, weights, ((2 * reach, 0),), slots)
    totals = settle(rows, [(mine, [(2 * reach, 0, False)])], shape)

    def slow(totals):
        more = products(tables, land, weights, tuple((e, half) for e in far), half)
        sent = [exchange(m, e) for m, e in zip(more, far)]
        return settle(rows, [(m, [(e, half, False)]) for m, e in zip(sent, far)], shape, totals)

    totals = lax.cond(flag > 0, slow, lambda totals: totals, totals)
    packed = pack(passed)
    returned = [across(packed, k, back=True) for k in range(1, ranks)]

    early = (near[0], near[1], far[0], far[1])
    totals = settle(rows, [(got[e], [(e, 0, False)]) for e in early], shape, totals)
    parts = [(got[e], [(e, 0, False)]) for e in (*near[2:], *far[2:])]
    parts += [(p, [(e, half, True)]) for p, e in zip(passed, far)]
    parts += [(r, [(e, half + k * piece, True) for e in far]) for k, r in enumerate(returned, 1)]
    totals = settle(rows, parts, shape, totals)
    totals = totals.reshape(kinds, AB_DEV, 2, steps, block_rows // 2).transpose(3, 0, 1, 2, 4)
    return totals.reshape(steps, kinds, AB_DEV * block_rows)


def solution(mesh):
    return jax.shard_map(
        on_device,
        mesh=mesh,
        in_specs=(
            P(None, None, None, AXES),
            P(None, AXES),
            P(AXES, None, None, None, None),
            P(AXES, None, None),
            P(AXES, None, None),
            P(AXES, None),
        ),
        out_specs=P(None, None, AXES),
        check_vma=False,
    )
```

time: 137 us -> 124 us (0.905); the launches traced: 137 us -> 123 us
  Pallas kernels: 0 us -> 26.6 us
  matrix products: 17.8 us -> 0 us
  waiting for transfers between devices: 61.6 us -> 50.5 us
  starting transfers between devices: 44.4 us -> 35.5 us
  local copies, waits for them, and re-layouts: 6.33 us -> 3.48 us
    pallas_call x0 -> x9, Pallas kernels: none -> 26.6 us  [the longest x3 10.1 us: products(): pl.pallas_call(functools.partial(product_kernel, chunks=chunks), grid_spe...]
    dot_general x8 -> x0, matrix products: 17.8 us -> none  [the longest x7 12 us: settle(): jnp.einsum('kj,kfr->jfr', onehot, partial_value, precision=lax.Precision....]
    ppermute x12 -> x20, waiting for transfers between devices: 61.6 us -> 50.5 us  [the longest x9 35 us: exchange(): lax.ppermute(value, AXES, [(d, (d + shifts[d % period][entry]) % count) f...]
    ppermute x12 -> x20, starting transfers between devices: 44.4 us -> 35.5 us  [the longest x9 16.6 us: exchange(): lax.ppermute(value, AXES, [(d, (d + shifts[d % period][entry]) % count) f...]
    reshape x2 -> x0, local copies, waits for them, and re-layouts: 4.82 us -> none  [on_device(): totals.transpose(1, 0, 2).reshape(num_steps, num_kinds, AB_DEV * block_rows)]
    reduce_sum x2 -> x3, other arithmetic: 4.9 us -> 0.45 us  [the longest x1 0.21 us: on_device(): numbers = jnp.sum(family[:ranks] >= 0, axis=2, dtype=jnp.int32)]
    unnamed x2 -> x16, local copies, waits for them, and re-layouts: 0.01 us -> 2.05 us
    concatenate x0 -> x6, other arithmetic: none -> 1.59 us  [the longest x4 0.79 us: spread(): held = jnp.concatenate([held, got], axis=0)]
  transfers between devices with their start and end apart: 12 -> 20, of which waited for: 4 -> 8; matrix products, arithmetic and copies ran while one was open for 6% -> 4% of each run, Pallas kernels for 0% -> 20%
where the time goes in v1:
time: 124 us; the launch traced here: 123 us
  waiting for transfers between devices  50.5 us (41%)
  starting transfers between devices  35.5 us (29%)
  Pallas kernels  26.6 us (21%)
  other arithmetic  5.61 us (5%)
  local copies, waits for them, and re-layouts  3.48 us (3%)
    ppermute x9, waiting for transfers between devices, exchange(): lax.ppermute(value, AXES, [(d, (d + shifts[d % period][entry]) % count) f...  35 us
    ppermute x9, starting transfers between devices, exchange(): lax.ppermute(value, AXES, [(d, (d + shifts[d % period][entry]) % count) f...  16.6 us
    ppermute x6, waiting for transfers between devices, across(): lax.ppermute(value, 'gx', [(b, a) for a, b in pairs] if back else pairs)  11.8 us
    pallas_call x3, Pallas kernels, products(): pl.pallas_call(functools.partial(product_kernel, chunks=chunks), grid_spe...  10.1 us
    ppermute x5, starting transfers between devices, spread(): got = lax.ppermute(held, axis, pairs)  9.92 us
    ppermute x6, starting transfers between devices, across(): lax.ppermute(value, 'gx', [(b, a) for a, b in pairs] if back else pairs)  8.96 us
    pallas_call x3, Pallas kernels, settle(): pl.pallas_call(functools.partial(settle_kernel, entries=tuple(entries), c...  6.43 us
    pallas_call x1, Pallas kernels, first_products(): pl.pallas_call(functools.partial(first_kernel, entries=entries, ranks=ran...  5.93 us
  transfers between devices with their start and end apart: 20, of which 8 were waited for; matrix products, arithmetic and copies ran while one was open for 4% of the time, Pallas kernels for 20%

profile of v1, /device:TPU:0, one launch (start us, length us, event | category | flops | bytes accessed | tf_op | source)
XLA Modules:
  0.0 122.5 jit_solution(7813617766916059211)
XLA Ops:
  0.0 0.8 compare_select_fusion
  0.8 3.0 %collective-permute-start.3 = (s32[1,7,16]{2,0,1:T(1,128)S(1)}, s32[1,7,16]{2,0,1:T(1,128)S(1)}, u32[]{:S(2)}, u32[]{:S(2)}) collective-permute-start(s32[1,7,16]{2,0,1:T(1,128)S(1)} %compare_select_fusion), channel_id=1, source_target_pairs={{0,8},{8,16},{16,24},{24,0},{1,9},{9,17},{17,25},{25,1},{2,10},{10... | collective-permute-start | bytes 1352 | tf_op jit(solution)/shard_map/ppermute | solution.py:324
  3.8 0.8 fusion.13
  4.5 0.7 fusion.12
  5.3 1.0 collective-permute-done.3
  6.3 2.1 %collective-permute-start.4 = (s32[2,7,16]{2,0,1:T(2,128)S(1)}, s32[2,7,16]{2,0,1:T(2,128)S(1)}, u32[]{:S(2)}, u32[]{:S(2)}) collective-permute-start(s32[2,7,16]{2,0,1:T(2,128)S(1)} %pad_add_fusion.4), channel_id=1, source_target_pairs={{0,16},{8,24},{16,0},{24,8},{1,17},{9,25},{17,1},{25,9},{2,18},{10... | collective-permute-start | bytes 2696 | tf_op jit(solution)/shard_map/ppermute | solution.py:324
  8.5 1.6 %collective-permute-done.4 = s32[2,7,16]{2,0,1:T(2,128)S(1)} collective-permute-done((s32[2,7,16]{2,0,1:T(2,128)S(1)}, s32[2,7,16]{2,0,1:T(2,128)S(1)}, u32[]{:S(2)}, u32[]{:S(2)}) %collective-permute-start.4) | collective-permute-done | bytes 928 | tf_op jit(solution)/shard_map/ppermute | solution.py:324
  10.0 0.2 convert_reduce_fusion
  10.3 0.1 convert_reduce_fusion.2
  10.4 0.6 and_reduce_fusion
  11.0 0.7 add_select_fusion
  11.8 1.2 collective-permute-done.5
  13.0 2.1 %collective-permute-start.6 = (s32[2,4,7,16]{3,1,2,0:T(4,128)S(1)}, s32[2,4,7,16]{3,1,2,0:T(4,128)S(1)}, u32[]{:S(2)}, u32[]{:S(2)}) collective-permute-start(s32[2,4,7,16]{3,1,2,0:T(4,128)S(1)} %pad_add_fusion.2), channel_id=1, source_target_pairs={{0,2},{1,3},{2,0},{3,1},{4,6},{5,7},{6,4},{7,5},{8,10},{9,11},{10,... | collective-permute-start | bytes 10760 | tf_op jit(solution)/shard_map/ppermute | solution.py:324
  15.1 5.9 %first.1 = (bf16[32,48,128]{2,1,0:T(8,128)(2,1)S(1)}, f32[8,48,256]{2,1,0:T(8,128)}, f32[8,48,256]{2,1,0:T(8,128)}, f32[8,48,256]{2,1,0:T(8,128)}, f32[3,2,48,25...) custom-call(s32[7]{0:T(128)S(1)} %get-tuple-element.61.offs_ref, ...), custom_call_target="tpu_custom_call" | custom-call | tf_op jit(solution)/shard_map/first/pallas_call | solution.py:137
  21.0 0.6 collective-permute-start.10
  21.7 1.5 %collective-permute-start.11 = (f32[3,2,48,256]{3,2,1,0:T(8,128)}, f32[3,2,48,256]{3,2,1,0:T(8,128)}, u32[]{:S(2)}, u32[]{:S(2)}) collective-permute-start(f32[3,2,48,256]{3,2,1,0:T(8,128)} %get-tuple-element.51), channel_id=1, source_target_pairs={{0,16},{8,24},{16,0},{24,8},{1,17},{9,25},{17,1},{25,9},{2,18},{10... | collective-permute-start | bytes 884744 | tf_op jit(solution)/shard_map/ppermute | solution.py:379
  23.2 2.7 %collective-permute-start.7 = (s32[4,4,7,16]{3,1,2,0:T(4,128)S(1)}, s32[4,4,7,16]{3,1,2,0:T(4,128)S(1)}, u32[]{:S(2)}, u32[]{:S(2)}) collective-permute-start(s32[4,4,7,16]{3,1,2,0:T(4,128)S(1)} %pad_add_fusion.1), channel_id=1, source_target_pairs={{0,4},{1,5},{2,6},{3,7},{4,0},{5,1},{6,2},{7,3},{8,12},{9,13},{10,... | collective-permute-start | bytes 21512 | tf_op jit(solution)/shard_map/ppermute | solution.py:324
  25.9 0.7 fusion.11
  26.6 3.0 %products.7.refs_0_ = f32[16,48,256]{2,1,0:T(8,128)} custom-call(s32[7]{0:T(128)S(1)} %get-tuple-element.61.offs_ref, s32[7,1,16]{2,1,0:T(1,128)S(1)} %bitcast.41, s32[1,7]{1,0:T(1,128)S(1)} %copy-done.10, bf16[32,48,128]{2,1,0:T(8,128)(2,1)S(1)} %get-tuple-element.46.land_ref, bf16[1,7,16,256,128]{4,3,2,1,0:T(8,128)(2,1)} %refs_0_.5), custom_call_target="tpu_custom_call" | custom-call | tf_op jit(solution)/shard_map/products/pallas_call | solution.py:175
  29.6 0.7 compare_reduce_fusion
  30.9 0.6 gather_fusion
  31.6 0.1 convert_reduce_fusion.1
  31.9 1.8 %settle.5 = f32[12,48,8,128]{3,2,1,0:T(8,128)S(1)} custom-call(s32[8,17]{1,0:T(8,128)S(1)} %concatenate.65.rows_ref, f32[16,48,256]{2,1,0:T(8,128)} %products.7.refs_0_), custom_call_target="tpu_custom_call" | custom-call | tf_op jit(solution)/shard_map/settle/pallas_call | solution.py:300
  33.7 2.7 %collective-permute-start.12 = (f32[3,2,48,256]{3,2,1,0:T(8,128)}, f32[3,2,48,256]{3,2,1,0:T(8,128)}, u32[]{:S(2)}, u32[]{:S(2)}) collective-permute-start(f32[3,2,48,256]{3,2,1,0:T(8,128)} %get-tuple-element.52), channel_id=1, source_target_pairs={{0,24},{8,0},{16,8},{24,16},{1,25},{9,1},{17,9},{25,17},{2,26},{10... | collective-permute-start | bytes 884744 | tf_op jit(solution)/shard_map/ppermute | solution.py:379
  36.4 3.1 %products.6 = f32[16,48,256]{2,1,0:T(8,128)} custom-call(s32[7]{0:T(128)S(1)} %get-tuple-element.61.offs_ref, s32[7,1,16]{2,1,0:T(1,128)S(1)} %bitcast.43, s32[1,7]{1,0:T(1,128)} %counts_ref.7, bf16[32,48,128]{2,1,0:T(8,128)(2,1)S(1)} %get-tuple-element.46.land_ref, bf16[1,7,16,256,128]{4,3,2,1,0:T(8,128)(2,1)} %refs_0_.5), custom_call_target="tpu_custom_call" | custom-call | tf_op jit(solution)/shard_map/products/pallas_call | solution.py:175
  39.5 0.6 collective-permute-start.20
  40.1 4.0 %products.5 = (f32[16,48,256]{2,1,0:T(8,128)}, f32[16,48,256]{2,1,0:T(8,128)}) custom-call(s32[7]{0:T(128)S(1)} %get-tuple-element.61.offs_ref, s32[7,1,16]{2,1,0:T(1,128)S(1)} %bitcast.44, s32[1,7]{1,0:T(1,128)} %counts_ref.7, bf16[32,48,128]{2,1,0:T(8,128)(2,1)S(1)} %get-tuple-element.46.land_ref, bf16[1,7,16,256,128]{4,3,2,1,0:T(8,128)(2,1)} %refs_0_.5, ...), custom_call_target="tpu_custom_call" | custom-call | tf_op jit(solution)/shard_map/products/pallas_call | solution.py:175
  44.1 0.6 copy.23.counts_ref
  44.7 2.5 %choose.1 = (f32[2,48,256]{2,1,0:T(8,128)}, f32[2,48,256]{2,1,0:T(8,128)}, f32[2,48,256]{2,1,0:T(8,128)}) custom-call(s32[7]{0:T(128)S(1)} %get-tuple-element.61.offs_ref, s32[4,7]{1,0:T(4,128)} %copy.23.counts_ref, f32[3,2,48,256]{3,2,1,0:T(8,128)} %get-tuple-element.49.refs_0_, f32[3,2,48,256]{3,2,1,0:T(8,128)} %collective-permute-done.10.refs_1_, ...), custom_call_target="tpu_custom_call" | custom-call | tf_op jit(solution)/shard_map/choose/pallas_call | solution.py:209
  47.2 0.9 collective-permute-start.13
  48.1 2.5 %collective-permute-start.14 = (f32[2,48,256]{2,1,0:T(8,128)}, f32[2,48,256]{2,1,0:T(8,128)S(1)}, u32[]{:S(2)}, u32[]{:S(2)}) collective-permute-start(f32[2,48,256]{2,1,0:T(8,128)} %get-tuple-element.54), channel_id=1, source_target_pairs={{0,30},{1,31},{2,4},{3,5},{4,2},{5,3},{6,8},{7,9},{8,6},{9,7},{10,... | collective-permute-start | bytes 294920 | tf_op jit(solution)/shard_map/ppermute | solution.py:375
  50.6 3.0 %collective-permute-start.15 = (f32[2,48,256]{2,1,0:T(8,128)}, f32[2,48,256]{2,1,0:T(8,128)S(1)}, u32[]{:S(2)}, u32[]{:S(2)}) collective-permute-start(f32[2,48,256]{2,1,0:T(8,128)} %get-tuple-element.55), channel_id=1, source_target_pairs={{0,31},{1,30},{2,5},{3,4},{4,3},{5,2},{6,9},{7,8},{8,7},{9,6},{10,... | collective-permute-start | bytes 294920 | tf_op jit(solution)/shard_map/ppermute | solution.py:375
  53.6 6.4 %collective-permute-done.13.refs_0_.refs_2_ = f32[2,48,256]{2,1,0:T(8,128)S(1)} collective-permute-done((f32[2,48,256]{2,1,0:T(8,128)}, f32[2,48,256]{2,1,0:T(8,128)S(1)}, u32[]{:S(2)}, u32[]{:S(2)}) %collective-permute-start.13) | collective-permute-done | bytes 98336 | tf_op jit(solution)/shard_map/ppermute | solution.py:375
  60.0 0.6 copy-done.6
  60.7 4.6 %collective-permute-start.21 = (f32[8,48,256]{2,1,0:T(8,128)}, f32[8,48,256]{2,1,0:T(8,128)S(1)}, u32[]{:S(2)}, u32[]{:S(2)}) collective-permute-start(f32[8,48,256]{2,1,0:T(8,128)} %get-tuple-element.57), channel_id=1, source_target_pairs={{0,29},{1,4},{2,31},{3,6},{4,1},{5,8},{6,3},{7,10},{8,5},{9,12},{1... | collective-permute-start | bytes 1179656 | tf_op jit(solution)/shard_map/ppermute | solution.py:375
  65.3 3.0 %collective-permute-start.22 = (f32[8,48,256]{2,1,0:T(8,128)}, f32[8,48,256]{2,1,0:T(8,128)}, u32[]{:S(2)}, u32[]{:S(2)}) collective-permute-start(f32[8,48,256]{2,1,0:T(8,128)} %get-tuple-element.58), channel_id=1, source_target_pairs={{0,30},{1,31},{2,4},{3,5},{4,2},{5,3},{6,8},{7,9},{8,6},{9,7},{10,... | collective-permute-start | bytes 1179656 | tf_op jit(solution)/shard_map/ppermute | solution.py:375
  68.2 13.7 %collective-permute-done.21.refs_2_ = f32[8,48,256]{2,1,0:T(8,128)S(1)} collective-permute-done((f32[8,48,256]{2,1,0:T(8,128)}, f32[8,48,256]{2,1,0:T(8,128)S(1)}, u32[]{:S(2)}, u32[]{:S(2)}) %collective-permute-start.21) | collective-permute-done | bytes 393248 | tf_op jit(solution)/shard_map/ppermute | solution.py:375
  82.0 2.1 %collective-permute-start.9 = (f32[8,48,256]{2,1,0:T(8,128)}, f32[8,48,256]{2,1,0:T(8,128)}, u32[]{:S(2)}, u32[]{:S(2)}) collective-permute-start(f32[8,48,256]{2,1,0:T(8,128)} %get-tuple-element.48), channel_id=1, source_target_pairs={{0,31},{1,30},{2,5},{3,4},{4,3},{5,2},{6,9},{7,8},{8,7},{9,6},{10,... | collective-permute-start | bytes 1179656 | tf_op jit(solution)/shard_map/ppermute | solution.py:375
  84.0 1.7 %pack.1 = f32[3,2,48,256]{3,2,1,0:T(8,128)} custom-call(f32[2,48,256]{2,1,0:T(8,128)} %copy-done.6, f32[2,48,256]{2,1,0:T(8,128)} %copy-done.7, f32[2,48,256]{2,1,0:T(8,128)} %copy-done.8), custom_call_target="tpu_custom_call" | custom-call | tf_op jit(solution)/shard_map/pack/pallas_call | solution.py:229
  85.7 14.8 %collective-permute-done.22.refs_3_ = f32[8,48,256]{2,1,0:T(8,128)} collective-permute-done((f32[8,48,256]{2,1,0:T(8,128)}, f32[8,48,256]{2,1,0:T(8,128)}, u32[]{:S(2)}, u32[]{:S(2)}) %collective-permute-start.22) | collective-permute-done | bytes 393248 | tf_op jit(solution)/shard_map/ppermute | solution.py:375
  100.6 1.6 %collective-permute-start.18 = (f32[3,2,48,256]{3,2,1,0:T(8,128)}, f32[3,2,48,256]{3,2,1,0:T(8,128)}, u32[]{:S(2)}, u32[]{:S(2)}) collective-permute-start(f32[3,2,48,256]{3,2,1,0:T(8,128)} %pack.1), channel_id=1, source_target_pairs={{24,0},{0,8},{8,16},{16,24},{25,1},{1,9},{9,17},{17,25},{26,2},{2,... | collective-permute-start | bytes 884744 | tf_op jit(solution)/shard_map/ppermute | solution.py:379
  102.2 0.4 collective-permute-start.17
  102.5 2.1 %collective-permute-start.16 = (f32[3,2,48,256]{3,2,1,0:T(8,128)}, f32[3,2,48,256]{3,2,1,0:T(8,128)}, u32[]{:S(2)}, u32[]{:S(2)}) collective-permute-start(f32[3,2,48,256]{3,2,1,0:T(8,128)} %pack.1), channel_id=1, source_target_pairs={{8,0},{16,8},{24,16},{0,24},{9,1},{17,9},{25,17},{1,25},{10,2},{18... | collective-permute-start | bytes 884744 | tf_op jit(solution)/shard_map/ppermute | solution.py:379
  104.7 2.3 %settle.6.refs_8_ = f32[12,48,8,128]{3,2,1,0:T(8,128)S(1)} custom-call(s32[8,17]{1,0:T(8,128)S(1)} %concatenate.65.rows_ref, f32[16,48,256]{2,1,0:T(8,128)} %collective-permute-done.19.refs_0_, f32[16,48,256]{2,1,0:T(8,128)} %copy-done.1, f32[8,48,256]{2,1,0:T(8,128)} %copy-done.2, ...), custom_call_target="tpu_custom_call", output_to_operand_aliasing={{}: (5, {})} | custom-call | tf_op jit(solution)/shard_map/settle/pallas_call | solution.py:300
  107.0 5.6 %collective-permute-done.18.refs_7_ = f32[3,2,48,256]{3,2,1,0:T(8,128)} collective-permute-done((f32[3,2,48,256]{3,2,1,0:T(8,128)}, f32[3,2,48,256]{3,2,1,0:T(8,128)}, u32[]{:S(2)}, u32[]{:S(2)}) %collective-permute-start.18) | collective-permute-done | bytes 294944 | tf_op jit(solution)/shard_map/ppermute | solution.py:379
  112.6 6.2 %collective-permute-done.17.refs_6_ = f32[3,2,48,256]{3,2,1,0:T(8,128)} collective-permute-done((f32[3,2,48,256]{3,2,1,0:T(8,128)}, f32[3,2,48,256]{3,2,1,0:T(8,128)}, u32[]{:S(2)}, u32[]{:S(2)}) %collective-permute-start.17) | collective-permute-done | bytes 294944 | tf_op jit(solution)/shard_map/ppermute | solution.py:379
  118.8 2.3 %settle.7 = f32[12,48,8,128]{3,2,1,0:T(8,128)S(1)} custom-call(s32[8,17]{1,0:T(8,128)S(1)} %concatenate.65.rows_ref, f32[16,48,256]{2,1,0:T(8,128)} %collective-permute-done.8.refs_0_, f32[8,48,256]{2,1,0:T(8,128)} %collective-permute-done.9.refs_1_, f32[2,48,256]{2,1,0:T(8,128)} %copy-done.6, ...), custom_call_target="tpu_custom_call", output_to_operand_aliasing={{}: (9, {})} | custom-call | tf_op jit(solution)/shard_map/settle/pallas_call | solution.py:300
  121.2 1.4 %copy-done = f32[12,48,8,128]{3,2,1,0:T(8,128)} copy-done((f32[12,48,8,128]{3,2,1,0:T(8,128)}, f32[12,48,8,128]{3,2,1,0:T(8,128)S(1)}, u32[]{:S(2)}) %copy-start) | copy-done | bytes 2359320
  (38 shorter events, 0.5 us)
Async XLA Ops:
  0.8 5.6 %collective-permute-start.3 = (s32[1,7,16]{2,0,1:T(1,128)S(1)}, s32[1,7,16]{2,0,1:T(1,128)S(1)}, u32[]{:S(2)}, u32[]{:S(2)}) collective-permute-start(s32[1,7,16]{2,0,1:T(1,128)S(1)} %compare_select_fusion), channel_id=1, source_target_pairs={{0,8},{8,16},{16,24},{24,0},{1,9},{9,17},{17,25},{25,1},{2,10},{10... | collective-permute-start | bytes 1352 | tf_op jit(solution)/shard_map/ppermute | solution.py:324
  6.3 3.7 %collective-permute-start.4 = (s32[2,7,16]{2,0,1:T(2,128)S(1)}, s32[2,7,16]{2,0,1:T(2,128)S(1)}, u32[]{:S(2)}, u32[]{:S(2)}) collective-permute-start(s32[2,7,16]{2,0,1:T(2,128)S(1)} %pad_add_fusion.4), channel_id=1, source_target_pairs={{0,16},{8,24},{16,0},{24,8},{1,17},{9,25},{17,1},{25,9},{2,18},{10... | collective-permute-start | bytes 2696 | tf_op jit(solution)/shard_map/ppermute | solution.py:324
  11.7 1.2 %collective-permute-start.5 = (s32[1,4,7,16]{3,1,2,0:T(4,128)S(1)}, s32[1,4,7,16]{3,1,2,0:T(4,128)S(1)}, u32[]{:S(2)}, u32[]{:S(2)}) collective-permute-start(s32[1,4,7,16]{3,1,2,0:T(4,128)S(1)} %add_select_fusion), channel_id=1, source_target_pairs={{0,1},{1,0},{2,3},{3,2},{4,5},{5,4},{6,7},{7,6},{8,9},{9,8},{10,11... | collective-permute-start | bytes 5384 | tf_op jit(solution)/shard_map/ppermute | solution.py:324
  13.0 10.2 %collective-permute-start.6 = (s32[2,4,7,16]{3,1,2,0:T(4,128)S(1)}, s32[2,4,7,16]{3,1,2,0:T(4,128)S(1)}, u32[]{:S(2)}, u32[]{:S(2)}) collective-permute-start(s32[2,4,7,16]{3,1,2,0:T(4,128)S(1)} %pad_add_fusion.2), channel_id=1, source_target_pairs={{0,2},{1,3},{2,0},{3,1},{4,6},{5,7},{6,4},{7,5},{8,10},{9,11},{10,... | collective-permute-start | bytes 10760 | tf_op jit(solution)/shard_map/ppermute | solution.py:324
  15.1 11.5 %copy-start.9 = (s32[1,7,16]{2,0,1:T(1,128)S(1)}, s32[1,7,16]{2,0,1:T(1,128)}, u32[]{:S(2)}) copy-start(s32[1,7,16]{2,0,1:T(1,128)} %param.13) | copy-start | bytes 1348
  15.1 11.5 %copy-start.10 = (s32[1,7]{1,0:T(1,128)S(1)}, s32[1,7]{1,0:T(1,128)}, u32[]{:S(2)}) copy-start(s32[1,7]{1,0:T(1,128)} %counts_ref.7) | copy-start | bytes 88
  21.0 23.7 %collective-permute-start.10 = (f32[3,2,48,256]{3,2,1,0:T(8,128)}, f32[3,2,48,256]{3,2,1,0:T(8,128)}, u32[]{:S(2)}, u32[]{:S(2)}) collective-permute-start(f32[3,2,48,256]{3,2,1,0:T(8,128)} %get-tuple-element.50), channel_id=1, source_target_pairs={{0,8},{8,16},{16,24},{24,0},{1,9},{9,17},{17,25},{25,1},{2,10},{10... | collective-permute-start | bytes 884744 | tf_op jit(solution)/shard_map/ppermute | solution.py:379
  21.7 23.0 %collective-permute-start.11 = (f32[3,2,48,256]{3,2,1,0:T(8,128)}, f32[3,2,48,256]{3,2,1,0:T(8,128)}, u32[]{:S(2)}, u32[]{:S(2)}) collective-permute-start(f32[3,2,48,256]{3,2,1,0:T(8,128)} %get-tuple-element.51), channel_id=1, source_target_pairs={{0,16},{8,24},{16,0},{24,8},{1,17},{9,25},{17,1},{25,9},{2,18},{10... | collective-permute-start | bytes 884744 | tf_op jit(solution)/shard_map/ppermute | solution.py:379
  23.2 6.4 %collective-permute-start.7 = (s32[4,4,7,16]{3,1,2,0:T(4,128)S(1)}, s32[4,4,7,16]{3,1,2,0:T(4,128)S(1)}, u32[]{:S(2)}, u32[]{:S(2)}) collective-permute-start(s32[4,4,7,16]{3,1,2,0:T(4,128)S(1)} %pad_add_fusion.1), channel_id=1, source_target_pairs={{0,4},{1,5},{2,6},{3,7},{4,0},{5,1},{6,2},{7,3},{8,12},{9,13},{10,... | collective-permute-start | bytes 21512 | tf_op jit(solution)/shard_map/ppermute | solution.py:324
  33.7 11.0 %collective-permute-start.12 = (f32[3,2,48,256]{3,2,1,0:T(8,128)}, f32[3,2,48,256]{3,2,1,0:T(8,128)}, u32[]{:S(2)}, u32[]{:S(2)}) collective-permute-start(f32[3,2,48,256]{3,2,1,0:T(8,128)} %get-tuple-element.52), channel_id=1, source_target_pairs={{0,24},{8,0},{16,8},{24,16},{1,25},{9,1},{17,9},{25,17},{2,26},{10... | collective-permute-start | bytes 884744 | tf_op jit(solution)/shard_map/ppermute | solution.py:379
  39.5 62.7 %collective-permute-start.20 = (f32[16,48,256]{2,1,0:T(8,128)}, f32[16,48,256]{2,1,0:T(8,128)S(1)}, u32[]{:S(2)}, u32[]{:S(2)}) collective-permute-start(f32[16,48,256]{2,1,0:T(8,128)} %products.6), channel_id=1, source_target_pairs={{0,2},{1,3},{2,0},{3,1},{4,6},{5,7},{6,4},{7,5},{8,10},{9,11},{10,... | collective-permute-start | bytes 2359304 | tf_op jit(solution)/shard_map/ppermute | solution.py:375
  44.1 58.5 %collective-permute-start.19 = (f32[16,48,256]{2,1,0:T(8,128)}, f32[16,48,256]{2,1,0:T(8,128)}, u32[]{:S(2)}, u32[]{:S(2)}) collective-permute-start(f32[16,48,256]{2,1,0:T(8,128)} %get-tuple-element.56), channel_id=1, source_target_pairs={{0,1},{1,0},{2,3},{3,2},{4,5},{5,4},{6,7},{7,6},{8,9},{9,8},{10,11... | collective-permute-start | bytes 2359304 | tf_op jit(solution)/shard_map/ppermute | solution.py:375
  47.2 12.9 %collective-permute-start.13 = (f32[2,48,256]{2,1,0:T(8,128)}, f32[2,48,256]{2,1,0:T(8,128)S(1)}, u32[]{:S(2)}, u32[]{:S(2)}) collective-permute-start(f32[2,48,256]{2,1,0:T(8,128)} %get-tuple-element.53), channel_id=1, source_target_pairs={{0,29},{1,4},{2,31},{3,6},{4,1},{5,8},{6,3},{7,10},{8,5},{9,12},{1... | collective-permute-start | bytes 294920 | tf_op jit(solution)/shard_map/ppermute | solution.py:375
  48.1 17.1 %collective-permute-start.14 = (f32[2,48,256]{2,1,0:T(8,128)}, f32[2,48,256]{2,1,0:T(8,128)S(1)}, u32[]{:S(2)}, u32[]{:S(2)}) collective-permute-start(f32[2,48,256]{2,1,0:T(8,128)} %get-tuple-element.54), channel_id=1, source_target_pairs={{0,30},{1,31},{2,4},{3,5},{4,2},{5,3},{6,8},{7,9},{8,6},{9,7},{10,... | collective-permute-start | bytes 294920 | tf_op jit(solution)/shard_map/ppermute | solution.py:375
  50.6 14.6 %collective-permute-start.15 = (f32[2,48,256]{2,1,0:T(8,128)}, f32[2,48,256]{2,1,0:T(8,128)S(1)}, u32[]{:S(2)}, u32[]{:S(2)}) collective-permute-start(f32[2,48,256]{2,1,0:T(8,128)} %get-tuple-element.55), channel_id=1, source_target_pairs={{0,31},{1,30},{2,5},{3,4},{4,3},{5,2},{6,9},{7,8},{8,7},{9,6},{10,... | collective-permute-start | bytes 294920 | tf_op jit(solution)/shard_map/ppermute | solution.py:375
  60.0 0.6 copy-start.6
  60.7 21.3 %collective-permute-start.21 = (f32[8,48,256]{2,1,0:T(8,128)}, f32[8,48,256]{2,1,0:T(8,128)S(1)}, u32[]{:S(2)}, u32[]{:S(2)}) collective-permute-start(f32[8,48,256]{2,1,0:T(8,128)} %get-tuple-element.57), channel_id=1, source_target_pairs={{0,29},{1,4},{2,31},{3,6},{4,1},{5,8},{6,3},{7,10},{8,5},{9,12},{1... | collective-permute-start | bytes 1179656 | tf_op jit(solution)/shard_map/ppermute | solution.py:375
  65.2 16.7 %copy-start.7 = (f32[2,48,256]{2,1,0:T(8,128)}, f32[2,48,256]{2,1,0:T(8,128)S(1)}, u32[]{:S(2)}) copy-start(f32[2,48,256]{2,1,0:T(8,128)S(1)} %collective-permute-done.14.refs_1_.refs_3_) | copy-start | bytes 294916
  65.2 53.6 %collective-permute-start.8 = (f32[16,48,256]{2,1,0:T(8,128)}, f32[16,48,256]{2,1,0:T(8,128)}, u32[]{:S(2)}, u32[]{:S(2)}) collective-permute-start(f32[16,48,256]{2,1,0:T(8,128)} %get-tuple-element.47), channel_id=1, source_target_pairs={{0,3},{1,2},{2,1},{3,0},{4,7},{5,6},{6,5},{7,4},{8,11},{9,10},{10,... | collective-permute-start | bytes 2359304 | tf_op jit(solution)/shard_map/ppermute | solution.py:375
  65.2 16.7 %copy-start.8 = (f32[2,48,256]{2,1,0:T(8,128)}, f32[2,48,256]{2,1,0:T(8,128)S(1)}, u32[]{:S(2)}) copy-start(f32[2,48,256]{2,1,0:T(8,128)S(1)} %collective-permute-done.15.refs_2_.refs_4_) | copy-start | bytes 294916
  65.3 35.3 %collective-permute-start.22 = (f32[8,48,256]{2,1,0:T(8,128)}, f32[8,48,256]{2,1,0:T(8,128)}, u32[]{:S(2)}, u32[]{:S(2)}) collective-permute-start(f32[8,48,256]{2,1,0:T(8,128)} %get-tuple-element.58), channel_id=1, source_target_pairs={{0,30},{1,31},{2,4},{3,5},{4,2},{5,3},{6,8},{7,9},{8,6},{9,7},{10,... | collective-permute-start | bytes 1179656 | tf_op jit(solution)/shard_map/ppermute | solution.py:375
  82.0 22.7 %copy-start.2 = (f32[8,48,256]{2,1,0:T(8,128)}, f32[8,48,256]{2,1,0:T(8,128)S(1)}, u32[]{:S(2)}) copy-start(f32[8,48,256]{2,1,0:T(8,128)S(1)} %collective-permute-done.21.refs_2_) | copy-start | bytes 1179652
  82.0 25.0 %collective-permute-start.9 = (f32[8,48,256]{2,1,0:T(8,128)}, f32[8,48,256]{2,1,0:T(8,128)}, u32[]{:S(2)}, u32[]{:S(2)}) collective-permute-start(f32[8,48,256]{2,1,0:T(8,128)} %get-tuple-element.48), channel_id=1, source_target_pairs={{0,31},{1,30},{2,5},{3,4},{4,3},{5,2},{6,9},{7,8},{8,7},{9,6},{10,... | collective-permute-start | bytes 1179656 | tf_op jit(solution)/shard_map/ppermute | solution.py:375
  100.6 12.1 %collective-permute-start.18 = (f32[3,2,48,256]{3,2,1,0:T(8,128)}, f32[3,2,48,256]{3,2,1,0:T(8,128)}, u32[]{:S(2)}, u32[]{:S(2)}) collective-permute-start(f32[3,2,48,256]{3,2,1,0:T(8,128)} %pack.1), channel_id=1, source_target_pairs={{24,0},{0,8},{8,16},{16,24},{25,1},{1,9},{9,17},{17,25},{26,2},{2,... | collective-permute-start | bytes 884744 | tf_op jit(solution)/shard_map/ppermute | solution.py:379
  102.2 2.5 %copy-start.1 = (f32[16,48,256]{2,1,0:T(8,128)}, f32[16,48,256]{2,1,0:T(8,128)S(1)}, u32[]{:S(2)}) copy-start(f32[16,48,256]{2,1,0:T(8,128)S(1)} %collective-permute-done.20.refs_1_) | copy-start | bytes 2359300
  102.2 16.6 %collective-permute-start.17 = (f32[3,2,48,256]{3,2,1,0:T(8,128)}, f32[3,2,48,256]{3,2,1,0:T(8,128)}, u32[]{:S(2)}, u32[]{:S(2)}) collective-permute-start(f32[3,2,48,256]{3,2,1,0:T(8,128)} %pack.1), channel_id=1, source_target_pairs={{16,0},{24,8},{0,16},{8,24},{17,1},{25,9},{1,17},{9,25},{18,2},{26... | collective-permute-start | bytes 884744 | tf_op jit(solution)/shard_map/ppermute | solution.py:379
  102.5 16.3 %collective-permute-start.16 = (f32[3,2,48,256]{3,2,1,0:T(8,128)}, f32[3,2,48,256]{3,2,1,0:T(8,128)}, u32[]{:S(2)}, u32[]{:S(2)}) collective-permute-start(f32[3,2,48,256]{3,2,1,0:T(8,128)} %pack.1), channel_id=1, source_target_pairs={{8,0},{16,8},{24,16},{0,24},{9,1},{17,9},{25,17},{1,25},{10,2},{18... | collective-permute-start | bytes 884744 | tf_op jit(solution)/shard_map/ppermute | solution.py:379
  121.1 1.4 %copy-start = (f32[12,48,8,128]{3,2,1,0:T(8,128)}, f32[12,48,8,128]{3,2,1,0:T(8,128)S(1)}, u32[]{:S(2)}) copy-start(f32[12,48,8,128]{3,2,1,0:T(8,128)S(1)} %settle.7) | copy-start | bytes 7077892

commit v2 on v1

--- a/solution.py
+++ b/solution.py
@@ -3,6 +3,7 @@
 
 import jax
 import jax.numpy as jnp
+import numpy as np
 from jax import lax
 from jax.experimental import pallas as pl
 from jax.experimental.pallas import tpu as pltpu
@@ -60,97 +61,102 @@
     )
 
 
-def first_kernel(offs_ref, cols_ref, counts_ref, flux, frac, weights, land_out, *refs, entries, ranks):
-    far = len(entries)
-    outs, refs = refs[: far + ranks], refs[far + ranks :]
-    flux_v, frac_v, w_v, land_v, near_v, piece_v, in_sems, w_sems, out_sems = refs
+def first_kernel(offs_ref, cols_ref, counts_ref, flux, frac, weights, land_out, *refs, far, near, ranks):
+    outs, refs = refs[: len(far) + 1 + ranks], refs[len(far) + 1 + ranks :]
+    flux_v, frac_v, w_v, land_v, far_v, near_v, piece_v, in_sems, w_sems, out_sems = refs
     groups, half = flux_v.shape[0], w_v.shape[1]
     wide = flux_v.shape[-1]
     piece = piece_v.shape[2]
     blocks = land_v.shape[0] // groups
+    chunks = [(e, 0, None) for e in far] + [(near, 0, None), (near, 1, None)] + [(e, 1, i) for i, e in enumerate(far)]
 
     def load_flux(i):
         return pltpu.make_async_copy(flux.at[:, :, :, pl.ds(i * wide, wide)], flux_v.at[i], in_sems.at[1 + i])
 
-    def load_weights(index, part):
-        source = weights.at[0, offs_ref[entries[index]], pl.ds(part * half, half)]
-        return pltpu.make_async_copy(source, w_v.at[part * far + index], w_sems.at[part * far + index])
-
-    def crowded(index):
-        return counts_ref[0, offs_ref[entries[index]]] > half
+    def load_weights(index):
+        entry, part, _ = chunks[index]
+        source = weights.at[0, offs_ref[entry], pl.ds(part * half, half)]
+        return pltpu.make_async_copy(source, w_v.at[index], w_sems.at[index])
+
+    def used(index):
+        entry, part, _ = chunks[index]
+        return counts_ref[0, offs_ref[entry]] > part * half
 
     load_frac = pltpu.make_async_copy(frac, frac_v, in_sems.at[0])
     load_frac.start()
     for i in range(groups):
         load_flux(i).start()
-    for index in range(far):
-        load_weights(index, 0).start()
-    for index in range(far):
-
-        @pl.when(crowded(index))
+    for index in range(len(chunks)):
+
+        @pl.when(used(index))
         def _():
-            load_weights(index, 1).start()
+            load_weights(index).start()
 
     load_frac.wait()
     for i in range(groups):
         load_flux(i).wait()
         merge_blocks(flux_v.at[i], frac_v, land_v, i * blocks, blocks)
-    stores = [pltpu.make_async_copy(land_v, land_out, out_sems.at[far + ranks])]
-    stores[0].start()
-    for index, entry in enumerate(entries):
-        load_weights(index, 0).wait()
-        for local in range(half):
-            near_v[index, local] = lax.dot_general(
-                land_v[cols_ref[offs_ref[entry], 0, local]],
-                w_v[index, local],
-                (((1,), (1,)), ((), ())),
-                preferred_element_type=jnp.float32,
-            )
-        stores.append(pltpu.make_async_copy(near_v.at[index], outs[index], out_sems.at[index]))
+    stores = []
+
+    def store(source, to):
+        stores.append(pltpu.make_async_copy(source, to, out_sems.at[len(stores)]))
         stores[-1].start()
-    for index, entry in enumerate(entries):
-
-        @pl.when(crowded(index))
+
+    store(land_v, land_out)
+    for index, (entry, part, at) in enumerate(chunks):
+
+        @pl.when(used(index))
         def _():
-            load_weights(index, 1).wait()
+            load_weights(index).wait()
             for local in range(half):
-                piece_v[local // piece, index, local % piece] = lax.dot_general(
-                    land_v[cols_ref[offs_ref[entry], 0, half + local]],
-                    w_v[far + index, local],
+                value = lax.dot_general(
+                    land_v[cols_ref[offs_ref[entry], 0, part * half + local]],
+                    w_v[index, local],
                     (((1,), (1,)), ((), ())),
                     preferred_element_type=jnp.float32,
                 )
-
+                if at is not None:
+                    piece_v[local // piece, at, local % piece] = value
+                elif entry == near:
+                    near_v[part * half + local] = value
+                else:
+                    far_v[index, local] = value
+
+        if index < len(far):
+            store(far_v.at[index], outs[index])
+        elif index == len(far) + 1:
+            store(near_v, outs[len(far)])
     for k in range(ranks):
-        stores.append(pltpu.make_async_copy(piece_v.at[k], outs[far + k], out_sems.at[far + k]))
-        stores[-1].start()
-    for store in stores:
-        store.wait()
-
-
-def first_products(tables, tile_flux, tile_frac, weights, entries, ranks, piece):
+        store(piece_v.at[k], outs[len(far) + 1 + k])
+    for copy in stores:
+        copy.wait()
+
+
+def first_products(tables, tile_flux, tile_frac, weights, far, near, ranks, piece):
     steps, kinds, tiles, cells = tile_flux.shape
     _, _, slots, rows, cols = weights.shape
-    nf, blocks, half, far = steps * kinds, cells // cols, slots // 2, len(entries)
+    nf, blocks, half = steps * kinds, cells // cols, slots // 2
     groups = min(g for g in range(1, blocks + 1) if blocks % g == 0 and blocks // g <= 4)
     anywhere = pl.BlockSpec(memory_space=pl.ANY)
+    shapes = [(half, nf, rows)] * len(far) + [(slots, nf, rows)] + [(len(far), piece, nf, rows)] * ranks
+    chunks = 2 * len(far) + 2
     return pl.pallas_call(
-        functools.partial(first_kernel, entries=entries, ranks=ranks),
+        functools.partial(first_kernel, far=far, near=near, ranks=ranks),
         in_specs=[pl.BlockSpec(memory_space=pltpu.SMEM)] * 3 + [anywhere] * 3,
-        out_specs=[anywhere] * (1 + far + ranks),
+        out_specs=[anywhere] * (1 + len(shapes)),
         out_shape=[jax.ShapeDtypeStruct((blocks, nf, cols), jnp.bfloat16)]
-        + [jax.ShapeDtypeStruct((half, nf, rows), jnp.float32) for _ in entries]
-        + [jax.ShapeDtypeStruct((far, piece, nf, rows), jnp.float32) for _ in range(ranks)],
+        + [jax.ShapeDtypeStruct(shape, jnp.float32) for shape in shapes],
         scratch_shapes=[
             pltpu.VMEM((groups, steps, kinds, tiles, cells // groups), tile_flux.dtype),
             pltpu.VMEM(tile_frac.shape, tile_frac.dtype),
-            pltpu.VMEM((2 * far, half, rows, cols), weights.dtype),
+            pltpu.VMEM((chunks, half, rows, cols), weights.dtype),
             pltpu.VMEM((blocks, nf, cols), jnp.bfloat16),
-            pltpu.VMEM((far, half, nf, rows), jnp.float32),
-            pltpu.VMEM((ranks, far, piece, nf, rows), jnp.float32),
+            pltpu.VMEM((len(far), half, nf, rows), jnp.float32),
+            pltpu.VMEM((slots, nf, rows), jnp.float32),
+            pltpu.VMEM((ranks, len(far), piece, nf, rows), jnp.float32),
             pltpu.SemaphoreType.DMA((1 + groups,)),
-            pltpu.SemaphoreType.DMA((2 * far,)),
-            pltpu.SemaphoreType.DMA((far + ranks + 1,)),
+            pltpu.SemaphoreType.DMA((chunks,)),
+            pltpu.SemaphoreType.DMA((1 + len(shapes),)),
         ],
         name="first",
     )(*tables, tile_flux, tile_frac, weights)
@@ -189,14 +195,14 @@
     )(*tables, land, *([weights] * len(chunks)))
 
 
-def choose_kernel(offs_ref, counts_ref, *refs, entries, half):
+def choose_kernel(offs_ref, info_ref, *refs, entries, half, places, at):
     ranks = len(refs) - 1 - len(entries)
     outs, sems = refs[ranks:-1], refs[-1]
     for go in (True, False):
         for index, entry in enumerate(entries):
             pick = jnp.int32(0)
             for rank in reversed(range(ranks)):
-                pick = jnp.where(counts_ref[rank, offs_ref[entry]] > half, rank, pick)
+                pick = jnp.where(info_ref[places[rank], at + offs_ref[entry]] > half, rank, pick)
             for rank in range(ranks):
 
                 @pl.when(pick == rank)
@@ -205,15 +211,15 @@
                     copy.start() if go else copy.wait()
 
 
-def choose(offs, counts, givens, entries, half):
+def choose(offs, info, givens, entries, half, places, at):
     return pl.pallas_call(
-        functools.partial(choose_kernel, entries=entries, half=half),
+        functools.partial(choose_kernel, entries=entries, half=half, places=places, at=at),
         in_specs=[pl.BlockSpec(memory_space=pltpu.SMEM)] * 2 + [pl.BlockSpec(memory_space=pl.ANY)] * len(givens),
         out_specs=[pl.BlockSpec(memory_space=pltpu.VMEM)] * len(entries),
         out_shape=[jax.ShapeDtypeStruct(givens[0].shape[1:], jnp.float32)] * len(entries),
         scratch_shapes=[pltpu.SemaphoreType.DMA((len(entries),))],
         name="choose",
-    )(offs, counts, *givens)
+    )(offs, info, *givens)
 
 
 def pack_kernel(*refs):
@@ -236,16 +242,59 @@
     )(*givens)
 
 
-def settle_kernel(rows_ref, *refs, entries, count, fresh):
+def add_block(totals, block, value):
+    kinds = totals.shape[0]
+    steps = totals.shape[2] // 2
+    low = lax.broadcasted_iota(jnp.int32, (2 * steps, LANES), 0) < steps
+    for pair in range(kinds // 2):
+        lines = pl.ds(pair * 2 * steps, 2 * steps)
+        left, right = value[lines, pl.ds(0, LANES)], value[lines, pl.ds(LANES, LANES)]
+        totals[2 * pair, block] += jnp.where(low, left, pltpu.roll(right, steps, 0))
+        totals[2 * pair + 1, block] += jnp.where(low, pltpu.roll(left, steps, 0), right)
+
+
+def own_kernel(cols_ref, rows_ref, counts_ref, land_ref, w_ref, totals, made, *, offset):
+    totals[...] = jnp.zeros(totals.shape, totals.dtype)
+    slots = made.shape[0]
+    for start in range(0, slots, SUBLANES):
+
+        @pl.when(start < counts_ref[0, offset])
+        def _():
+            for local in range(start, min(start + SUBLANES, slots)):
+                made[local] = block_product(land_ref, cols_ref[offset, 0, local], w_ref, local)
+
+    @pl.loop(0, counts_ref[0, offset])
+    def _(slot):
+        add_block(totals, rows_ref[offset, 0, slot], made.at[slot])
+
+
+def own_totals(block_col, block_row, counts, land, weights, offset, shape):
+    _, _, slots, rows, cols = weights.shape
+    smem = pl.BlockSpec(memory_space=pltpu.SMEM)
+    return pl.pallas_call(
+        functools.partial(own_kernel, offset=offset),
+        grid=(1,),
+        in_specs=[smem] * 3
+        + [
+            pl.BlockSpec(land.shape, lambda i: (0, 0, 0)),
+            pl.BlockSpec((1, 1, slots, rows, cols), lambda i: (0, offset, 0, 0, 0)),
+        ],
+        out_specs=pl.BlockSpec(shape, lambda i: (0, 0, 0, 0)),
+        out_shape=jax.ShapeDtypeStruct(shape, jnp.float32),
+        scratch_shapes=[pltpu.VMEM((slots, land.shape[1], rows), jnp.float32)],
+        name="own",
+    )(block_col, block_row, counts, land, weights)
+
+
+def settle_kernel(where_ref, flag_ref, info_ref, *refs, entries, count, fresh, slots, at):
     rest = refs[count:]
     given = None if fresh else rest[0]
     out, totals, held, sems, moves = rest[-5:]
-    last = rows_ref.shape[0] - 1
 
     def live(entry):
         _, _, row, first, limit, _, fast = entries[entry]
-        number = jnp.clip(rows_ref[row, 0] - first, 0, limit)
-        return jnp.where(rows_ref[last, 0] > 0, 0, number) if fast else number
+        number = jnp.clip(info_ref[where_ref[0, row], at + where_ref[1, row]] - first, 0, limit)
+        return jnp.where(flag_ref[0] > 0, 0, number) if fast else number
 
     def copy(entry, slot):
         index, sub, place = entries[entry][0], entries[entry][1], entries[entry][5]
@@ -264,29 +313,21 @@
         load = pltpu.make_async_copy(given, totals, moves.at[0])
         load.start()
         load.wait()
-    kinds = totals.shape[0]
-    steps = totals.shape[2] // 2
-    low = lax.broadcasted_iota(jnp.int32, (2 * steps, LANES), 0) < steps
     for entry in range(len(entries)):
 
         @pl.loop(0, live(entry))
         def _(slot, entry=entry):
             copy(entry, slot).wait()
             _, _, row, first, _, start, _ = entries[entry]
-            block = rows_ref[row, 1 + first + slot]
-            for pair in range(kinds // 2):
-                lines = pl.ds(pair * 2 * steps, 2 * steps)
-                left = held[start + slot, lines, pl.ds(0, LANES)]
-                right = held[start + slot, lines, pl.ds(LANES, LANES)]
-                totals[2 * pair, block] += jnp.where(low, left, pltpu.roll(right, steps, 0))
-                totals[2 * pair + 1, block] += jnp.where(low, pltpu.roll(left, steps, 0), right)
+            block = info_ref[where_ref[0, row], where_ref[1, row] * slots + first + slot]
+            add_block(totals, block, held.at[start + slot])
 
     store = pltpu.make_async_copy(totals, out, moves.at[1])
     store.start()
     store.wait()
 
 
-def settle(rows, parts, shape, totals=None):
+def settle(tables, parts, shape, slots, at, totals=None):
     fresh = totals is None
     arrays = [array for array, _ in parts]
     entries, place = [], 0
@@ -298,8 +339,10 @@
     count = len(arrays)
     given = [] if fresh else [totals]
     return pl.pallas_call(
-        functools.partial(settle_kernel, entries=tuple(entries), count=count, fresh=fresh),
-        in_specs=[pl.BlockSpec(memory_space=pltpu.SMEM)]
+        functools.partial(
+            settle_kernel, entries=tuple(entries), count=count, fresh=fresh, slots=slots, at=at
+        ),
+        in_specs=[pl.BlockSpec(memory_space=pltpu.SMEM)] * 3
         + [pl.BlockSpec(memory_space=pl.ANY) for _ in arrays]
         + [pl.BlockSpec(memory_space=pl.ANY) for _ in given],
         out_specs=pl.BlockSpec(memory_space=pl.ANY),
@@ -310,26 +353,35 @@
             pltpu.SemaphoreType.DMA((place,)),
             pltpu.SemaphoreType.DMA((2,)),
         ],
-        input_output_aliases={} if fresh else {1 + count: 0},
+        input_output_aliases={} if fresh else {3 + count: 0},
         name="settle",
-    )(rows, *arrays, *given)
-
-
-def spread(held, axis, paired=False):
-    size = lax.axis_size(axis)
-    held = held[None]
-    span = 1
-    while span < size:
+    )(*tables, *arrays, *given)
+
+
+def spans(axis, size):
+    return [(axis, 1 << bit) for bit in range((size - 1).bit_length())]
+
+
+def rounds_of(ranks, line):
+    gx, gy = spans("gx", ranks), spans("gy", line)
+    return gy[:-1] + gx + gy[-1:]
+
+
+def spread(held, rounds, *ready):
+    known = []
+    for axis, span in rounds:
+        size = lax.axis_size(axis)
+        paired = axis == "gy" and size & (size - 1) == 0
         pairs = [(d, d ^ span if paired else (d + span) % size) for d in range(size)]
         got = lax.ppermute(held, axis, pairs)
+        got = lax.optimization_barrier((got, *ready))[0]
         held = jnp.concatenate([held, got], axis=0)
-        span *= 2
-    return held
-
-
-def place_of(axis, other, paired=False):
-    own = lax.axis_index(axis)
-    return own ^ other if paired else (own - other) % lax.axis_size(axis)
+        known.append(held)
+    return known
+
+
+def place_of(rounds, back, along):
+    return sum((((back if axis == "gx" else along) & span) != 0) * (1 << bit) for bit, (axis, span) in enumerate(rounds))
 
 
 def partners(reach):
@@ -378,54 +430,59 @@
         pairs = [(r, (r + step) % ranks) for r in range(ranks)]
         return lax.ppermute(value, "gx", [(b, a) for a, b in pairs] if back else pairs)
 
-    codes = jnp.where(jnp.arange(slots)[None, :] < send_counts[0][:, None], block_row[0], -1)
-    family = spread(codes, "gx")
-    numbers = jnp.sum(family[:ranks] >= 0, axis=2, dtype=jnp.int32)
-    outside = jnp.any(jnp.arange(num_off)[:, None] == offs[None, reach : 2 * reach], axis=1)
-    crowded = jnp.any((jnp.sum(numbers > half, axis=0) > 1) & outside)
-    family = jnp.where(crowded & (family >= 0), family + AB_DEV, family)
-
-    land, *given = first_products(tables, tile_flux, tile_frac, weights, far, ranks, piece)
-    outer, parts = given[: len(far)], given[len(far) :]
-    middle = near[1:2]
-    inner = {}
-    for those in (middle, tuple(e for e in near if e not in middle)):
-        inner.update(zip(those, products(tables, land, weights, tuple((e, 0) for e in those), slots)))
+    at = num_off * slots
+    info = jnp.concatenate([block_row.reshape(1, at), send_counts], axis=1)
+    rounds = rounds_of(ranks, line)
+    family = spread(info, rounds[:-1])[-1]
+    places = tuple(place_of(rounds, k, 0) for k in range(ranks))
+
+    land, *given = first_products(tables, tile_flux, tile_frac, weights, far, near[1], ranks, piece)
+    outer, parts = given[: len(far)], given[len(far) + 1 :]
+    those = tuple(e for e in near if e != near[1])
+    inner = dict(zip(those, products(tables, land, weights, tuple((e, 0) for e in those), slots)))
+    inner[near[1]] = given[len(far)]
 
     got = {e: exchange(outer[e - reach], e) for e in far}
     lent = [parts[0]] + [across(parts[k], k) for k in range(1, ranks)]
     got.update({e: exchange(inner[e], e) for e in near})
-    relay = choose(offs, numbers, lent, far, half)
+    relay = choose(offs, family, lent, far, half, places, at)
     passed = [exchange(r, e) for r, e in zip(relay, far)]
-    paired = line & (line - 1) == 0
-    held = spread(family, "gy", paired)
+    packed = pack(passed)
+    returned = [across(packed, k, back=True) for k in range(1, ranks)]
+
+    (held,) = spread(family, rounds[-1:], packed)
 
     sender = (rank * line + here + shift_here) % count
     back_offs = num_off - 1 - offs
-    rows = held[place_of("gy", sender % line, paired), place_of("gx", sender // line), back_offs]
-    flag = jnp.any(held >= AB_DEV).astype(jnp.int32)
-    lives = jnp.sum(rows >= 0, axis=1, keepdims=True, dtype=jnp.int32)
-    rows = jnp.concatenate([lives, rows % AB_DEV], axis=1)
-    rows = jnp.concatenate([rows, jnp.broadcast_to(flag, (1, rows.shape[1]))], axis=0)
-
-    (mine,) = products(tables, land, weights, ((2 * reach, 0),), slots)
-    totals = settle(rows, [(mine, [(2 * reach, 0, False)])], shape)
+    paired = line & (line - 1) == 0
+
+    def along(place):
+        return here ^ place if paired else (here - place) % line
+
+    where = jnp.stack([place_of(rounds, (rank - sender // line) % ranks, along(sender % line)), back_offs])
+    pick = np.zeros((line, held.shape[0]), np.float32)
+    for y in range(line):
+        pick[y, [place_of(rounds, k, y) for k in range(ranks)]] = 1
+    outside = [[v in row[reach:] for v in range(-reach, reach + 1)] for row in shifts]
+    spots = [[outside[(p ^ y if paired else p - y) % period] for y in range(line)] for p in range(period)]
+    many = jnp.dot(pick, (held[:, at:] > half).astype(jnp.float32))
+    flag = jnp.any((many > 1.5) & jnp.array(spots)[here % period]).astype(jnp.int32).reshape(1)
+    settled = (where, flag, held)
+
+    totals = own_totals(tables[1], block_row.transpose(1, 0, 2), send_counts, land, weights, reach, shape)
 
     def slow(totals):
         more = products(tables, land, weights, tuple((e, half) for e in far), half)
         sent = [exchange(m, e) for m, e in zip(more, far)]
-        return settle(rows, [(m, [(e, half, False)]) for m, e in zip(sent, far)], shape, totals)
-
-    totals = lax.cond(flag > 0, slow, lambda totals: totals, totals)
-    packed = pack(passed)
-    returned = [across(packed, k, back=True) for k in range(1, ranks)]
-
+        return settle(settled, [(m, [(e, half, False)]) for m, e in zip(sent, far)], shape, slots, at, totals)
+
+    totals = lax.cond(flag[0] > 0, slow, lambda totals: totals, totals)
     early = (near[0], near[1], far[0], far[1])
-    totals = settle(rows, [(got[e], [(e, 0, False)]) for e in early], shape, totals)
+    totals = settle(settled, [(got[e], [(e, 0, False)]) for e in early], shape, slots, at, totals)
     parts = [(got[e], [(e, 0, False)]) for e in (*near[2:], *far[2:])]
     parts += [(p, [(e, half, True)]) for p, e in zip(passed, far)]
     parts += [(r, [(e, half + k * piece, True) for e in far]) for k, r in enumerate(returned, 1)]
-    totals = settle(rows, parts, shape, totals)
+    totals = settle(settled, parts, shape, slots, at, totals)
     totals = totals.reshape(kinds, AB_DEV, 2, steps, block_rows // 2).transpose(3, 0, 1, 2, 4)
     return totals.reshape(steps, kinds, AB_DEV * block_rows)
 

time: 124 us -> 135 us (1.089)
  waiting for transfers between devices: 50.5 us -> 69.3 us
  starting transfers between devices: 35.5 us -> 30.1 us
  Pallas kernels: 26.6 us -> 21.5 us
  local copies, waits for them, and re-layouts: 3.48 us -> 7.83 us
  other arithmetic: 5.61 us -> 2.93 us
  matrix products: 0 us -> 1.54 us
    ppermute x9, waiting for transfers between devices: 35 us -> 47 us  [exchange(): lax.ppermute(value, AXES, [(d, (d + shifts[d % period][entry]) % count) f...]
    pallas_call x3 -> x1, Pallas kernels: 10.1 us -> 3.89 us  [products(): pl.pallas_call(functools.partial(product_kernel, chunks=chunks), grid_spe...]
    ppermute x5, waiting for transfers between devices: 3.74 us -> 9.73 us  [spread(): got = lax.ppermute(held, axis, pairs)]
    ppermute x5, starting transfers between devices: 9.92 us -> 4.47 us  [spread(): got = lax.ppermute(held, axis, pairs)]
    concatenate x1 -> x2, local copies, waits for them, and re-layouts: 0.01 us -> 3.28 us  [spread(): held = jnp.concatenate([held, got], axis=0)]
    pallas_call x1 -> x2, Pallas kernels: 5.93 us -> 8.19 us  [the longest x1 6.54 us: first_products(): pl.pallas_call(functools.partial(first_kernel, far=far, near=near, ranks=...]
    ppermute x9, starting transfers between devices: 16.6 us -> 18.4 us  [exchange(): lax.ppermute(value, AXES, [(d, (d + shifts[d % period][entry]) % count) f...]
    ppermute x6, starting transfers between devices: 8.96 us -> 7.15 us  [across(): lax.ppermute(value, 'gx', [(b, a) for a, b in pairs] if back else pairs)]
  transfers between devices with their start and end apart: 20 -> 20, of which waited for: 8 -> 11; matrix products, arithmetic and copies ran while one was open for 4% -> 6% of each run, Pallas kernels for 20% -> 14%
where the time goes in v2:
time: 135 us; the launch traced here: 134 us
  waiting for transfers between devices  69.3 us (51%)
  starting transfers between devices  30.1 us (22%)
  Pallas kernels  21.5 us (16%)
  local copies, waits for them, and re-layouts  7.83 us (6%)
  other arithmetic  2.93 us (2%)
  matrix products  1.54 us (1%)
    ppermute x9, waiting for transfers between devices, exchange(): lax.ppermute(value, AXES, [(d, (d + shifts[d % period][entry]) % count) f...  47 us
    ppermute x9, starting transfers between devices, exchange(): lax.ppermute(value, AXES, [(d, (d + shifts[d % period][entry]) % count) f...  18.4 us
    ppermute x6, waiting for transfers between devices, across(): lax.ppermute(value, 'gx', [(b, a) for a, b in pairs] if back else pairs)  12.6 us
    ppermute x5, waiting for transfers between devices, spread(): got = lax.ppermute(held, axis, pairs)  9.73 us
    ppermute x6, starting transfers between devices, across(): lax.ppermute(value, 'gx', [(b, a) for a, b in pairs] if back else pairs)  7.15 us
    pallas_call x1, Pallas kernels, first_products(): pl.pallas_call(functools.partial(first_kernel, far=far, near=near, ranks=...  6.54 us
    pallas_call x2, Pallas kernels, settle(): pl.pallas_call(functools.partial(settle_kernel, entries=tuple(entries), c...  5.16 us
    ppermute x5, starting transfers between devices, spread(): got = lax.ppermute(held, axis, pairs)  4.47 us
  transfers between devices with their start and end apart: 20, of which 11 were waited for; matrix products, arithmetic and copies ran while one was open for 6% of the time, Pallas kernels for 14%

profile of v2, /device:TPU:0, one launch (start us, length us, event | category | flops | bytes accessed | tf_op | source)
XLA Modules:
  0.0 134.0 jit_solution(11668855617474018049)
XLA Ops:
  0.0 0.7 reduce
  0.7 0.1 reshape.14
  0.8 0.7 pad_add_fusion.4
  1.5 0.5 collective-permute-start.3
  2.0 0.7 fusion.14
  2.8 6.5 %first.1 = (bf16[32,48,128]{2,1,0:T(8,128)(2,1)S(1)}, f32[8,48,256]{2,1,0:T(8,128)}, f32[8,48,256]{2,1,0:T(8,128)}, f32[8,48,256]{2,1,0:T(8,128)}, f32[16,48,256...) custom-call(s32[7]{0:T(128)S(1)} %get-tuple-element.69.offs_ref, ...), custom_call_target="tpu_custom_call" | custom-call | tf_op jit(solution)/shard_map/first/pallas_call | solution.py:143
  9.3 3.5 %collective-permute-start.10 = (f32[3,2,48,256]{3,2,1,0:T(8,128)}, f32[3,2,48,256]{3,2,1,0:T(8,128)S(1)}, u32[]{:S(2)}, u32[]{:S(2)}) collective-permute-start(f32[3,2,48,256]{3,2,1,0:T(8,128)} %get-tuple-element.57), channel_id=1, source_target_pairs={{0,24},{8,0},{16,8},{24,16},{1,25},{9,1},{17,9},{25,17},{2,26},{10... | collective-permute-start | bytes 884744 | tf_op jit(solution)/shard_map/ppermute | solution.py:431
  12.8 1.1 collective-permute-start.9
  14.0 1.6 %collective-permute-start.4 = (s32[2,119]{1,0:T(2,128)S(1)}, s32[2,119]{1,0:T(2,128)S(1)}, u32[]{:S(2)}, u32[]{:S(2)}) collective-permute-start(s32[2,119]{1,0:T(2,128)S(1)} %pad_add_fusion.3), channel_id=1, source_target_pairs={{0,2},{1,3},{2,0},{3,1},{4,6},{5,7},{6,4},{7,5},{8,10},{9,11},{10,... | collective-permute-start | bytes 2864 | tf_op jit(solution)/shard_map/ppermute | solution.py:376
  15.6 2.0 %collective-permute-done.4 = s32[2,119]{1,0:T(2,128)S(1)} collective-permute-done((s32[2,119]{1,0:T(2,128)S(1)}, s32[2,119]{1,0:T(2,128)S(1)}, u32[]{:S(2)}, u32[]{:S(2)}) %collective-permute-start.4) | collective-permute-done | bytes 984 | tf_op jit(solution)/shard_map/ppermute | solution.py:376
  17.7 2.4 %collective-permute-start.5 = (s32[4,119]{1,0:T(4,128)S(1)}, s32[4,119]{1,0:T(4,128)S(1)}, u32[]{:S(2)}, u32[]{:S(2)}) collective-permute-start(s32[4,119]{1,0:T(4,128)S(1)} %pad_add_fusion.1), channel_id=1, source_target_pairs={{0,8},{8,16},{16,24},{24,0},{1,9},{9,17},{17,25},{25,1},{2,10},{10... | collective-permute-start | bytes 5720 | tf_op jit(solution)/shard_map/ppermute | solution.py:376
  20.1 7.7 %collective-permute-done.5 = s32[4,119]{1,0:T(4,128)S(1)} collective-permute-done((s32[4,119]{1,0:T(4,128)S(1)}, s32[4,119]{1,0:T(4,128)S(1)}, u32[]{:S(2)}, u32[]{:S(2)}) %collective-permute-start.5) | collective-permute-done | bytes 1936 | tf_op jit(solution)/shard_map/ppermute | solution.py:376
  27.8 0.1 pad_add_fusion
  27.9 3.9 %products.3 = (f32[16,48,256]{2,1,0:T(8,128)}, f32[16,48,256]{2,1,0:T(8,128)}) custom-call(s32[7]{0:T(128)S(1)} %get-tuple-element.69.offs_ref, s32[7,1,16]{2,1,0:T(1,128)S(1)} %bitcast.21, s32[1,7]{1,0:T(1,128)S(1)} %copy-done.13, bf16[32,48,128]{2,1,0:T(8,128)(2,1)S(1)} %get-tuple-element.62.land_ref, bf16[1,7,16,256,128]{4,3,2,1,0:T(8,128)(2,1)} %w_ref.1, ...), custom_call_target="tpu_custom_call" | custom-call | tf_op jit(solution)/shard_map/products/pallas_call | solution.py:181
  31.8 1.7 %collective-permute-start.20 = (f32[16,48,256]{2,1,0:T(8,128)}, f32[16,48,256]{2,1,0:T(8,128)}, u32[]{:S(2)}, u32[]{:S(2)}) collective-permute-start(f32[16,48,256]{2,1,0:T(8,128)} %get-tuple-element.66), channel_id=1, source_target_pairs={{0,2},{1,3},{2,0},{3,1},{4,6},{5,7},{6,4},{7,5},{8,10},{9,11},{10,... | collective-permute-start | bytes 2359304 | tf_op jit(solution)/shard_map/ppermute | solution.py:427
  33.5 1.2 concatenate.26.info_ref
  34.8 0.7 copy-done.9
  35.5 0.1 copy-done.10
  35.6 0.1 copy-done.11
  35.7 2.6 %choose.1 = (f32[2,48,256]{2,1,0:T(8,128)}, f32[2,48,256]{2,1,0:T(8,128)}, f32[2,48,256]{2,1,0:T(8,128)}) custom-call(s32[7]{0:T(128)S(1)} %get-tuple-element.69.offs_ref, s32[16,119]{1,0:T(8,128)} %concatenate.26.info_ref, f32[3,2,48,256]{3,2,1,0:T(8,128)} %get-tuple-element.54.refs_0_, f32[3,2,48,256]{3,2,1,0:T(8,128)} %copy-done.10, ...), custom_call_target="tpu_custom_call" | custom-call | tf_op jit(solution)/shard_map/choose/pallas_call | solution.py:215
  38.3 4.2 %collective-permute-start.11 = (f32[2,48,256]{2,1,0:T(8,128)}, f32[2,48,256]{2,1,0:T(8,128)S(1)}, u32[]{:S(2)}, u32[]{:S(2)}) collective-permute-start(f32[2,48,256]{2,1,0:T(8,128)} %get-tuple-element.58), channel_id=1, source_target_pairs={{0,29},{1,4},{2,31},{3,6},{4,1},{5,8},{6,3},{7,10},{8,5},{9,12},{1... | collective-permute-start | bytes 294920 | tf_op jit(solution)/shard_map/ppermute | solution.py:427
  42.5 0.7 dynamic-slice_bitcast_fusion
  43.2 2.9 %collective-permute-start.12 = (f32[2,48,256]{2,1,0:T(8,128)}, f32[2,48,256]{2,1,0:T(8,128)}, u32[]{:S(2)}, u32[]{:S(2)}) collective-permute-start(f32[2,48,256]{2,1,0:T(8,128)} %get-tuple-element.59), channel_id=1, source_target_pairs={{0,30},{1,31},{2,4},{3,5},{4,2},{5,3},{6,8},{7,9},{8,6},{9,7},{10,... | collective-permute-start | bytes 294920 | tf_op jit(solution)/shard_map/ppermute | solution.py:427
  46.1 7.8 %collective-permute-done.11.refs_0_.refs_2_ = f32[2,48,256]{2,1,0:T(8,128)S(1)} collective-permute-done((f32[2,48,256]{2,1,0:T(8,128)}, f32[2,48,256]{2,1,0:T(8,128)S(1)}, u32[]{:S(2)}, u32[]{:S(2)}) %collective-permute-start.11) | collective-permute-done | bytes 98336 | tf_op jit(solution)/shard_map/ppermute | solution.py:427
  53.9 3.0 %collective-permute-start.13 = (f32[2,48,256]{2,1,0:T(8,128)}, f32[2,48,256]{2,1,0:T(8,128)}, u32[]{:S(2)}, u32[]{:S(2)}) collective-permute-start(f32[2,48,256]{2,1,0:T(8,128)} %get-tuple-element.60), channel_id=1, source_target_pairs={{0,31},{1,30},{2,5},{3,4},{4,3},{5,2},{6,9},{7,8},{8,7},{9,6},{10,... | collective-permute-start | bytes 294920 | tf_op jit(solution)/shard_map/ppermute | solution.py:427
  56.8 0.6 pad_add_fusion.2.where_ref
  57.4 1.7 %own.1 = f32[12,48,8,128]{3,2,1,0:T(8,128)S(1)} custom-call(s32[7,1,16]{2,1,0:T(1,128)S(1)} %bitcast.22, s32[7,1,16]{2,1,0:T(1,128)} %bitcast.23, s32[1,7]{1,0:T(1,128)S(1)} %copy-done.13, bf16[32,48,128]{2,1,0:T(8,128)(2,1)S(1)} %get-tuple-element.62.land_ref, bf16[1,7,16,256,128]{4,3,2,1,0:T(8,128)(2,1)} %w_ref.1), custom_call_target="tpu_custom_call" | custom-call | tf_op jit(solution)/shard_map/own/pallas_call | solution.py:274
  59.0 0.7 copy.13
  59.7 0.7 collective-permute-done.12.refs_1_.refs_3_
  60.4 2.2 %collective-permute-done.13.refs_2_.refs_4_ = f32[2,48,256]{2,1,0:T(8,128)} collective-permute-done((f32[2,48,256]{2,1,0:T(8,128)}, f32[2,48,256]{2,1,0:T(8,128)}, u32[]{:S(2)}, u32[]{:S(2)}) %collective-permute-start.13) | collective-permute-done | bytes 98336 | tf_op jit(solution)/shard_map/ppermute | solution.py:427
  62.6 1.7 %pack.1 = f32[3,2,48,256]{3,2,1,0:T(8,128)} custom-call(f32[2,48,256]{2,1,0:T(8,128)} %copy-done.8, f32[2,48,256]{2,1,0:T(8,128)} %collective-permute-done.12.refs_1_.refs_3_, f32[2,48,256]{2,1,0:T(8,128)} %collective-permute-done.13.refs_2_.refs_4_), custom_call_target="tpu_custom_call" | custom-call | tf_op jit(solution)/shard_map/pack/pallas_call | solution.py:235
  64.3 2.1 %concatenate.27.info_ref = s32[32,119]{1,0:T(8,128)S(1)} concatenate(s32[1,119]{1,0:T(1,128)} %copy-done.19, s32[1,119]{1,0:T(1,128)} %copy-done.18, s32[2,119]{1,0:T(2,128)} %copy-done.15, s32[4,119]{1,0:T(4,128)} %copy-done.14, s32[8,119]{1,0:T(8,128)} %copy-done.16, s32[16,119]{1,0:T(8,128)} %collective-permute-done.7), dimensions={0} | concatenate | bytes 30464 | tf_op jit(solution)/shard_map/concatenate | solution.py:378
  66.4 1.5 %fusion.2 = pred[]{:T(512)} fusion(pred[8,7]{0,1:T(8,128)(4,1)} %copy.13, bf16[8,32]{1,0:T(8,128)(2,1)} %constant.137, s32[32,119]{1,0:T(8,128)S(1)} %concatenate.27.info_ref), kind=kOutput, calls=%fused_computation.3 | convolution fusion | flops 4199 | bytes 15801 | tf_op jit(solution)/shard_map/dot_general | solution.py:468
  68.5 2.7 %collective-permute-start.21 = (f32[8,48,256]{2,1,0:T(8,128)}, f32[8,48,256]{2,1,0:T(8,128)S(1)}, u32[]{:S(2)}, u32[]{:S(2)}) collective-permute-start(f32[8,48,256]{2,1,0:T(8,128)} %get-tuple-element.67), channel_id=1, source_target_pairs={{0,29},{1,4},{2,31},{3,6},{4,1},{5,8},{6,3},{7,10},{8,5},{9,12},{1... | collective-permute-start | bytes 1179656 | tf_op jit(solution)/shard_map/ppermute | solution.py:427
  71.2 3.3 %collective-permute-start.22 = (f32[8,48,256]{2,1,0:T(8,128)}, f32[8,48,256]{2,1,0:T(8,128)S(1)}, u32[]{:S(2)}, u32[]{:S(2)}) collective-permute-start(f32[8,48,256]{2,1,0:T(8,128)} %get-tuple-element.68), channel_id=1, source_target_pairs={{0,30},{1,31},{2,4},{3,5},{4,2},{5,3},{6,8},{7,9},{8,6},{9,7},{10,... | collective-permute-start | bytes 1179656 | tf_op jit(solution)/shard_map/ppermute | solution.py:427
  74.5 16.9 %collective-permute-done.21.refs_2_ = f32[8,48,256]{2,1,0:T(8,128)S(1)} collective-permute-done((f32[8,48,256]{2,1,0:T(8,128)}, f32[8,48,256]{2,1,0:T(8,128)S(1)}, u32[]{:S(2)}, u32[]{:S(2)}) %collective-permute-start.21) | collective-permute-done | bytes 393248 | tf_op jit(solution)/shard_map/ppermute | solution.py:427
  91.4 0.8 copy-done.6
  92.2 0.6 collective-permute-start.15
  92.8 15.7 %collective-permute-done.22.refs_3_ = f32[8,48,256]{2,1,0:T(8,128)S(1)} collective-permute-done((f32[8,48,256]{2,1,0:T(8,128)}, f32[8,48,256]{2,1,0:T(8,128)S(1)}, u32[]{:S(2)}, u32[]{:S(2)}) %collective-permute-start.22) | collective-permute-done | bytes 393248 | tf_op jit(solution)/shard_map/ppermute | solution.py:427
  108.5 1.5 %collective-permute-start.16 = (f32[3,2,48,256]{3,2,1,0:T(8,128)}, f32[3,2,48,256]{3,2,1,0:T(8,128)}, u32[]{:S(2)}, u32[]{:S(2)}) collective-permute-start(f32[3,2,48,256]{3,2,1,0:T(8,128)} %pack.1), channel_id=1, source_target_pairs={{8,0},{16,8},{24,16},{0,24},{9,1},{17,9},{25,17},{1,25},{10,2},{18... | collective-permute-start | bytes 884744 | tf_op jit(solution)/shard_map/ppermute | solution.py:431
  110.0 1.1 collective-permute-start.18
  111.0 2.5 %settle.4.refs_8_ = f32[12,48,8,128]{3,2,1,0:T(8,128)S(1)} custom-call(s32[2,7]{1,0:T(2,128)} %pad_add_fusion.2.where_ref, s32[1]{0:T(128)} %bitcast.4.flag_ref, s32[32,119]{1,0:T(8,128)S(1)} %concatenate.27.info_ref, f32[16,48,256]{2,1,0:T(8,128)} %copy-done.1, f32[16,48,256]{2,1,0:T(8,128)} %collective-permute-done.20.refs_1_, ...), custom_call_target="tpu_custom_call", output_to_operand_aliasing={{}: (7, {})} | custom-call | tf_op jit(solution)/shard_map/settle/pallas_call | solution.py:341
  113.6 3.7 %collective-permute-done.15.refs_1_ = f32[8,48,256]{2,1,0:T(8,128)S(1)} collective-permute-done((f32[8,48,256]{2,1,0:T(8,128)}, f32[8,48,256]{2,1,0:T(8,128)S(1)}, u32[]{:S(2)}, u32[]{:S(2)}) %collective-permute-start.15) | collective-permute-done | bytes 393248 | tf_op jit(solution)/shard_map/ppermute | solution.py:427
  117.3 5.9 %collective-permute-done.16.refs_5_ = f32[3,2,48,256]{3,2,1,0:T(8,128)} collective-permute-done((f32[3,2,48,256]{3,2,1,0:T(8,128)}, f32[3,2,48,256]{3,2,1,0:T(8,128)}, u32[]{:S(2)}, u32[]{:S(2)}) %collective-permute-start.16) | collective-permute-done | bytes 294944 | tf_op jit(solution)/shard_map/ppermute | solution.py:431
  123.2 0.5 collective-permute-done.17.refs_6_
  123.7 6.2 %collective-permute-done.18.refs_7_ = f32[3,2,48,256]{3,2,1,0:T(8,128)} collective-permute-done((f32[3,2,48,256]{3,2,1,0:T(8,128)}, f32[3,2,48,256]{3,2,1,0:T(8,128)}, u32[]{:S(2)}, u32[]{:S(2)}) %collective-permute-start.18) | collective-permute-done | bytes 294944 | tf_op jit(solution)/shard_map/ppermute | solution.py:431
  129.9 2.6 %settle.5 = f32[12,48,8,128]{3,2,1,0:T(8,128)S(1)} custom-call(s32[2,7]{1,0:T(2,128)} %pad_add_fusion.2.where_ref, s32[1]{0:T(128)} %bitcast.4.flag_ref, s32[32,119]{1,0:T(8,128)S(1)} %concatenate.27.info_ref, f32[16,48,256]{2,1,0:T(8,128)} %collective-permute-done.14.refs_0_, f32[8,48,256]{2,1,0:T(8,128)} %copy-done.5, ...), custom_call_target="tpu_custom_call", output_to_operand_aliasing={{}: (11, {})} | custom-call | tf_op jit(solution)/shard_map/settle/pallas_call | solution.py:341
  132.6 1.4 %copy-done = f32[12,48,8,128]{3,2,1,0:T(8,128)} copy-done((f32[12,48,8,128]{3,2,1,0:T(8,128)}, f32[12,48,8,128]{3,2,1,0:T(8,128)S(1)}, u32[]{:S(2)}) %copy-start) | copy-done | bytes 2359320
  (47 shorter events, 0.3 us)
Async XLA Ops:
  1.5 32.0 %copy-start.19 = (s32[1,119]{1,0:T(1,128)}, s32[1,119]{1,0:T(1,128)S(1)}, u32[]{:S(2)}) copy-start(s32[1,119]{1,0:T(1,128)S(1)} %pad_add_fusion.4) | copy-start | bytes 1432
  1.5 12.4 %collective-permute-start.3 = (s32[1,119]{1,0:T(1,128)S(1)}, s32[1,119]{1,0:T(1,128)S(1)}, u32[]{:S(2)}, u32[]{:S(2)}) collective-permute-start(s32[1,119]{1,0:T(1,128)S(1)} %pad_add_fusion.4), channel_id=1, source_target_pairs={{0,1},{1,0},{2,3},{3,2},{4,5},{5,4},{6,7},{7,6},{8,9},{9,8},{10,11... | collective-permute-start | bytes 1436 | tf_op jit(solution)/shard_map/ppermute | solution.py:376
  2.7 32.0 %copy-start.17 = (s32[7]{0:T(128)}, s32[7]{0:T(128)S(1)}, u32[]{:S(2)}) copy-start(s32[7]{0:T(128)S(1)} %get-tuple-element.69.offs_ref) | copy-start | bytes 88
  2.7 11.2 %copy-start.13 = (s32[1,7]{1,0:T(1,128)S(1)}, s32[1,7]{1,0:T(1,128)}, u32[]{:S(2)}) copy-start(s32[1,7]{1,0:T(1,128)} %counts_ref.5) | copy-start | bytes 88
  2.8 25.1 %copy-start.12 = (s32[1,7,16]{2,0,1:T(1,128)S(1)}, s32[1,7,16]{2,0,1:T(1,128)}, u32[]{:S(2)}) copy-start(s32[1,7,16]{2,0,1:T(1,128)} %param.15) | copy-start | bytes 1348
  9.3 25.4 %collective-permute-start.10 = (f32[3,2,48,256]{3,2,1,0:T(8,128)}, f32[3,2,48,256]{3,2,1,0:T(8,128)S(1)}, u32[]{:S(2)}, u32[]{:S(2)}) collective-permute-start(f32[3,2,48,256]{3,2,1,0:T(8,128)} %get-tuple-element.57), channel_id=1, source_target_pairs={{0,24},{8,0},{16,8},{24,16},{1,25},{9,1},{17,9},{25,17},{2,26},{10... | collective-permute-start | bytes 884744 | tf_op jit(solution)/shard_map/ppermute | solution.py:431
  12.8 21.9 %collective-permute-start.8 = (f32[3,2,48,256]{3,2,1,0:T(8,128)}, f32[3,2,48,256]{3,2,1,0:T(8,128)S(1)}, u32[]{:S(2)}, u32[]{:S(2)}) collective-permute-start(f32[3,2,48,256]{3,2,1,0:T(8,128)} %get-tuple-element.55), channel_id=1, source_target_pairs={{0,8},{8,16},{16,24},{24,0},{1,9},{9,17},{17,25},{25,1},{2,10},{10... | collective-permute-start | bytes 884744 | tf_op jit(solution)/shard_map/ppermute | solution.py:431
  12.8 21.9 %collective-permute-start.9 = (f32[3,2,48,256]{3,2,1,0:T(8,128)}, f32[3,2,48,256]{3,2,1,0:T(8,128)S(1)}, u32[]{:S(2)}, u32[]{:S(2)}) collective-permute-start(f32[3,2,48,256]{3,2,1,0:T(8,128)} %get-tuple-element.56), channel_id=1, source_target_pairs={{0,16},{8,24},{16,0},{24,8},{1,17},{9,25},{17,1},{25,9},{2,18},{10... | collective-permute-start | bytes 884744 | tf_op jit(solution)/shard_map/ppermute | solution.py:431
  13.9 19.6 %copy-start.18 = (s32[1,119]{1,0:T(1,128)}, s32[1,119]{1,0:T(1,128)S(1)}, u32[]{:S(2)}) copy-start(s32[1,119]{1,0:T(1,128)S(1)} %collective-permute-done.3) | copy-start | bytes 1432
  14.0 3.6 %collective-permute-start.4 = (s32[2,119]{1,0:T(2,128)S(1)}, s32[2,119]{1,0:T(2,128)S(1)}, u32[]{:S(2)}, u32[]{:S(2)}) collective-permute-start(s32[2,119]{1,0:T(2,128)S(1)} %pad_add_fusion.3), channel_id=1, source_target_pairs={{0,2},{1,3},{2,0},{3,1},{4,6},{5,7},{6,4},{7,5},{8,10},{9,11},{10,... | collective-permute-start | bytes 2864 | tf_op jit(solution)/shard_map/ppermute | solution.py:376
  17.6 15.9 %copy-start.15 = (s32[2,119]{1,0:T(2,128)}, s32[2,119]{1,0:T(2,128)S(1)}, u32[]{:S(2)}) copy-start(s32[2,119]{1,0:T(2,128)S(1)} %collective-permute-done.4) | copy-start | bytes 2860
  17.7 10.1 %collective-permute-start.5 = (s32[4,119]{1,0:T(4,128)S(1)}, s32[4,119]{1,0:T(4,128)S(1)}, u32[]{:S(2)}, u32[]{:S(2)}) collective-permute-start(s32[4,119]{1,0:T(4,128)S(1)} %pad_add_fusion.1), channel_id=1, source_target_pairs={{0,8},{8,16},{16,24},{24,0},{1,9},{9,17},{17,25},{25,1},{2,10},{10... | collective-permute-start | bytes 5720 | tf_op jit(solution)/shard_map/ppermute | solution.py:376
  27.8 5.8 %copy-start.14 = (s32[4,119]{1,0:T(4,128)}, s32[4,119]{1,0:T(4,128)S(1)}, u32[]{:S(2)}) copy-start(s32[4,119]{1,0:T(4,128)S(1)} %collective-permute-done.5) | copy-start | bytes 5716
  27.8 3.9 %collective-permute-start.6 = (s32[8,119]{1,0:T(8,128)S(1)}, s32[8,119]{1,0:T(8,128)S(1)}, u32[]{:S(2)}, u32[]{:S(2)}) collective-permute-start(s32[8,119]{1,0:T(8,128)S(1)} %pad_add_fusion), channel_id=1, source_target_pairs={{0,16},{8,24},{16,0},{24,8},{1,17},{9,25},{17,1},{25,9},{2,18},{10... | collective-permute-start | bytes 11432 | tf_op jit(solution)/shard_map/ppermute | solution.py:376
  31.8 78.2 %collective-permute-start.19 = (f32[16,48,256]{2,1,0:T(8,128)}, f32[16,48,256]{2,1,0:T(8,128)S(1)}, u32[]{:S(2)}, u32[]{:S(2)}) collective-permute-start(f32[16,48,256]{2,1,0:T(8,128)} %get-tuple-element.65), channel_id=1, source_target_pairs={{0,1},{1,0},{2,3},{3,2},{4,5},{5,4},{6,7},{7,6},{8,9},{9,8},{10,11... | collective-permute-start | bytes 2359304 | tf_op jit(solution)/shard_map/ppermute | solution.py:427
  31.8 25.6 %copy-start.16 = (s32[8,119]{1,0:T(8,128)}, s32[8,119]{1,0:T(8,128)S(1)}, u32[]{:S(2)}) copy-start(s32[8,119]{1,0:T(8,128)S(1)} %collective-permute-done.6) | copy-start | bytes 11428
  31.8 78.2 %collective-permute-start.20 = (f32[16,48,256]{2,1,0:T(8,128)}, f32[16,48,256]{2,1,0:T(8,128)}, u32[]{:S(2)}, u32[]{:S(2)}) collective-permute-start(f32[16,48,256]{2,1,0:T(8,128)} %get-tuple-element.66), channel_id=1, source_target_pairs={{0,2},{1,3},{2,0},{3,1},{4,6},{5,7},{6,4},{7,5},{8,10},{9,11},{10,... | collective-permute-start | bytes 2359304 | tf_op jit(solution)/shard_map/ppermute | solution.py:427
  34.7 0.7 copy-start.9
  34.7 0.8 copy-start.10
  34.8 0.9 copy-start.11
  38.3 15.6 %collective-permute-start.11 = (f32[2,48,256]{2,1,0:T(8,128)}, f32[2,48,256]{2,1,0:T(8,128)S(1)}, u32[]{:S(2)}, u32[]{:S(2)}) collective-permute-start(f32[2,48,256]{2,1,0:T(8,128)} %get-tuple-element.58), channel_id=1, source_target_pairs={{0,29},{1,4},{2,31},{3,6},{4,1},{5,8},{6,3},{7,10},{8,5},{9,12},{1... | collective-permute-start | bytes 294920 | tf_op jit(solution)/shard_map/ppermute | solution.py:427
  43.2 21.1 %collective-permute-start.7 = (s32[16,119]{1,0:T(8,128)}, s32[16,119]{1,0:T(8,128)}, u32[]{:S(2)}, u32[]{:S(2)}) collective-permute-start(s32[16,119]{1,0:T(8,128)} %concatenate.26.info_ref), channel_id=1, source_target_pairs={{0,4},{1,5},{2,6},{3,7},{4,0},{5,1},{6,2},{7,3},{8,12},{9,13},{10,... | collective-permute-start | bytes 22856 | tf_op jit(solution)/shard_map/ppermute | solution.py:376
  43.2 17.2 %collective-permute-start.12 = (f32[2,48,256]{2,1,0:T(8,128)}, f32[2,48,256]{2,1,0:T(8,128)}, u32[]{:S(2)}, u32[]{:S(2)}) collective-permute-start(f32[2,48,256]{2,1,0:T(8,128)} %get-tuple-element.59), channel_id=1, source_target_pairs={{0,30},{1,31},{2,4},{3,5},{4,2},{5,3},{6,8},{7,9},{8,6},{9,7},{10,... | collective-permute-start | bytes 294920 | tf_op jit(solution)/shard_map/ppermute | solution.py:427
  53.9 3.5 %copy-start.8 = (f32[2,48,256]{2,1,0:T(8,128)}, f32[2,48,256]{2,1,0:T(8,128)S(1)}, u32[]{:S(2)}) copy-start(f32[2,48,256]{2,1,0:T(8,128)S(1)} %collective-permute-done.11.refs_0_.refs_2_) | copy-start | bytes 294916
  53.9 8.7 %collective-permute-start.13 = (f32[2,48,256]{2,1,0:T(8,128)}, f32[2,48,256]{2,1,0:T(8,128)}, u32[]{:S(2)}, u32[]{:S(2)}) collective-permute-start(f32[2,48,256]{2,1,0:T(8,128)} %get-tuple-element.60), channel_id=1, source_target_pairs={{0,31},{1,30},{2,5},{3,4},{4,3},{5,2},{6,9},{7,8},{8,7},{9,6},{10,... | collective-permute-start | bytes 294920 | tf_op jit(solution)/shard_map/ppermute | solution.py:427
  68.5 22.9 %collective-permute-start.21 = (f32[8,48,256]{2,1,0:T(8,128)}, f32[8,48,256]{2,1,0:T(8,128)S(1)}, u32[]{:S(2)}, u32[]{:S(2)}) collective-permute-start(f32[8,48,256]{2,1,0:T(8,128)} %get-tuple-element.67), channel_id=1, source_target_pairs={{0,29},{1,4},{2,31},{3,6},{4,1},{5,8},{6,3},{7,10},{8,5},{9,12},{1... | collective-permute-start | bytes 1179656 | tf_op jit(solution)/shard_map/ppermute | solution.py:427
  71.2 58.7 %collective-permute-start.14 = (f32[16,48,256]{2,1,0:T(8,128)}, f32[16,48,256]{2,1,0:T(8,128)}, u32[]{:S(2)}, u32[]{:S(2)}) collective-permute-start(f32[16,48,256]{2,1,0:T(8,128)} %get-tuple-element.63), channel_id=1, source_target_pairs={{0,3},{1,2},{2,1},{3,0},{4,7},{5,6},{6,5},{7,4},{8,11},{9,10},{10,... | collective-permute-start | bytes 2359304 | tf_op jit(solution)/shard_map/ppermute | solution.py:427
  71.2 37.2 %collective-permute-start.22 = (f32[8,48,256]{2,1,0:T(8,128)}, f32[8,48,256]{2,1,0:T(8,128)S(1)}, u32[]{:S(2)}, u32[]{:S(2)}) collective-permute-start(f32[8,48,256]{2,1,0:T(8,128)} %get-tuple-element.68), channel_id=1, source_target_pairs={{0,30},{1,31},{2,4},{3,5},{4,2},{5,3},{6,8},{7,9},{8,6},{9,7},{10,... | collective-permute-start | bytes 1179656 | tf_op jit(solution)/shard_map/ppermute | solution.py:427
  91.4 0.8 copy-start.6
  92.2 25.2 %collective-permute-start.15 = (f32[8,48,256]{2,1,0:T(8,128)}, f32[8,48,256]{2,1,0:T(8,128)S(1)}, u32[]{:S(2)}, u32[]{:S(2)}) collective-permute-start(f32[8,48,256]{2,1,0:T(8,128)} %get-tuple-element.64), channel_id=1, source_target_pairs={{0,31},{1,30},{2,5},{3,4},{4,3},{5,2},{6,9},{7,8},{8,7},{9,6},{10,... | collective-permute-start | bytes 1179656 | tf_op jit(solution)/shard_map/ppermute | solution.py:427
  108.5 1.5 %copy-start.7 = (f32[8,48,256]{2,1,0:T(8,128)}, f32[8,48,256]{2,1,0:T(8,128)S(1)}, u32[]{:S(2)}) copy-start(f32[8,48,256]{2,1,0:T(8,128)S(1)} %collective-permute-done.22.refs_3_) | copy-start | bytes 1179652
  108.5 14.7 %collective-permute-start.16 = (f32[3,2,48,256]{3,2,1,0:T(8,128)}, f32[3,2,48,256]{3,2,1,0:T(8,128)}, u32[]{:S(2)}, u32[]{:S(2)}) collective-permute-start(f32[3,2,48,256]{3,2,1,0:T(8,128)} %pack.1), channel_id=1, source_target_pairs={{8,0},{16,8},{24,16},{0,24},{9,1},{17,9},{25,17},{1,25},{10,2},{18... | collective-permute-start | bytes 884744 | tf_op jit(solution)/shard_map/ppermute | solution.py:431
  110.0 1.1 copy-start.1
  110.0 13.7 %collective-permute-start.17 = (f32[3,2,48,256]{3,2,1,0:T(8,128)}, f32[3,2,48,256]{3,2,1,0:T(8,128)}, u32[]{:S(2)}, u32[]{:S(2)}) collective-permute-start(f32[3,2,48,256]{3,2,1,0:T(8,128)} %pack.1), channel_id=1, source_target_pairs={{16,0},{24,8},{0,16},{8,24},{17,1},{25,9},{1,17},{9,25},{18,2},{26... | collective-permute-start | bytes 884744 | tf_op jit(solution)/shard_map/ppermute | solution.py:431
  110.0 19.9 %collective-permute-start.18 = (f32[3,2,48,256]{3,2,1,0:T(8,128)}, f32[3,2,48,256]{3,2,1,0:T(8,128)}, u32[]{:S(2)}, u32[]{:S(2)}) collective-permute-start(f32[3,2,48,256]{3,2,1,0:T(8,128)} %pack.1), channel_id=1, source_target_pairs={{24,0},{0,8},{8,16},{16,24},{25,1},{1,9},{9,17},{17,25},{26,2},{2,... | collective-permute-start | bytes 884744 | tf_op jit(solution)/shard_map/ppermute | solution.py:431
  117.3 12.6 %copy-start.5 = (f32[8,48,256]{2,1,0:T(8,128)}, f32[8,48,256]{2,1,0:T(8,128)S(1)}, u32[]{:S(2)}) copy-start(f32[8,48,256]{2,1,0:T(8,128)S(1)} %collective-permute-done.15.refs_1_) | copy-start | bytes 1179652
  132.6 1.4 %copy-start = (f32[12,48,8,128]{3,2,1,0:T(8,128)}, f32[12,48,8,128]{3,2,1,0:T(8,128)S(1)}, u32[]{:S(2)}) copy-start(f32[12,48,8,128]{3,2,1,0:T(8,128)S(1)} %settle.5) | copy-start | bytes 7077892
